TPU v7x, 32 devices: a whole 2x2x4 slice. The times are simulated.
32 devices in a mesh: tp: 4 (over y, x), dp: 8 (over z, core).
Axes of the slice: x: 2, y: 2, z: 4, core: 2. Of those that a mesh axis runs over, the one named last changes fastest.
Arguments:
- activations: bfloat16 [2, 8192, 8192], P(None, 'dp', 'tp'), may hold values from -72 to 72
- out_grads: bfloat16 [2, 8192, 2048], P(None, 'dp'), may hold values from -2 to 2
- master: float32 [8192, 2, 2048], P(('tp', 'dp')), may hold values from -1.2 to 1.2
- first_moment: float32 [8192, 2, 2048], P(('tp', 'dp')), may hold values from -1.8 to 1.8
- second_moment: float32 [8192, 2, 2048], P(('tp', 'dp')), may hold values from 0.01 to 1
Outputs:
- new_master: float32 [8192, 2, 2048], P(('tp', 'dp'))
- new_first: float32 [8192, 2, 2048], P(('tp', 'dp'))
- new_second: float32 [8192, 2, 2048], P(('tp', 'dp'))
- weights: bfloat16 [8192, 2, 2048], P('tp')
All inputs are finite; a program needn't handle non-finite values.
Results may differ from a plain program's by a relative error of at most 0.0004.
Values may be sent and summed in bfloat16 or wider, within the bound.
A program may use at most 192 MiB of HBM per device.

v0:
```python
import functools
import math

import jax
import jax.numpy as jnp
from jax import lax
from jax.experimental import pallas as pl
from jax.experimental.layout import Layout, with_layout_constraint
from jax.experimental.pallas import tpu as pltpu
from jax.sharding import PartitionSpec as P

beta_first = 0.9
beta_second = 0.95
first_fix = 1.0 - 0.9**10
second_fix = 1.0 - 0.95**10
learn_rate = 0.01
decay_rate = 0.1
epsilon = 1e-08
limit_scale = 2.0
MESH = pl.DeviceIdType.MESH


def total_kernel(n_tp, n_dp, value_ref, total_ref, held, send_sem, recv_sem):
    count = n_tp * n_dp
    me = lax.axis_index("tp") * n_dp + lax.axis_index("dp")

    def device(k):
        other = lax.rem(me + k, count)
        return {"tp": other // n_dp, "dp": lax.rem(other, n_dp)}

    def copy(k, slot):
        return pltpu.make_async_remote_copy(
            src_ref=value_ref,
            dst_ref=held.at[slot],
            send_sem=send_sem.at[k],
            recv_sem=recv_sem.at[k],
            device_id=device(k),
            device_id_type=MESH,
        )

    barrier = pltpu.get_barrier_semaphore()

    @pl.loop(1, count)
    def _(k):
        pl.semaphore_signal(barrier, inc=1, device_id=device(k), device_id_type=MESH)

    pl.semaphore_wait(barrier, count - 1)

    @pl.loop(1, count)
    def _(k):
        copy(k, me).start()

    held[me] = value_ref[...]

    @pl.loop(1, count)
    def _(k):
        copy(k, lax.rem(me - k + count, count)).wait()

    total_ref[0] = jnp.sum(held[...], axis=0)
    total_ref[1] = jnp.sum(held[pl.ds(lax.axis_index("tp") * n_dp, n_dp)], axis=0)


def device_total(value):
    n_tp, n_dp = lax.axis_size("tp"), lax.axis_size("dp")
    count = n_tp * n_dp
    total = pl.pallas_call(
        functools.partial(total_kernel, n_tp, n_dp),
        out_shape=jax.ShapeDtypeStruct((2, 8, 128), jnp.float32),
        in_specs=[pl.BlockSpec(memory_space=pltpu.VMEM)],
        out_specs=pl.BlockSpec(memory_space=pltpu.VMEM),
        scratch_shapes=[
            pltpu.VMEM((count, 8, 128), jnp.float32),
            pltpu.SemaphoreType.DMA((count,)),
            pltpu.SemaphoreType.DMA((count,)),
        ],
        compiler_params=pltpu.CompilerParams(collective_id=0, has_side_effects=True),
        name="device_total",
    )(jnp.full((8, 128), value, jnp.float32))
    return total[0, 0, 0], total[1, 0, 0]


def reduce_rows(activations, out_grads):
    n_dp = lax.axis_size("dp")
    cores = 2 if n_dp % 2 == 0 else 1
    chips = n_dp // cores
    index = lax.axis_index("dp")
    chip, core = index // cores, lax.rem(index, cores)
    layers, tokens, width = activations.shape
    rows = width // n_dp

    def longest(x):
        squares = jnp.sum(jnp.square(x.astype(jnp.float32)), axis=1)
        return jnp.sqrt(jnp.max(squares))

    _, bound = device_total(longest(activations) * longest(out_grads))
    bound = jnp.maximum(1.001 * bound, 1e-25)
    shrink, grow = 250.0 / bound, bound / 250.0

    def pack(x):
        x = x * shrink
        return (x * jnp.abs(x)).astype(jnp.float16)

    def unpack(x):
        x = x.astype(jnp.float32)
        return jnp.sign(x) * jnp.sqrt(jnp.abs(x)) * grow

    swap = [(i, i // cores * cores + (i + 1) % cores) for i in range(n_dp)]
    ways = [1 if layer % 2 == 0 else -1 for layer in range(layers)]
    rings = [[(i, (i + way * cores) % n_dp) for i in range(n_dp)] for way in ways]

    def product(acts, layer, which, half):
        start = (which * cores + half) * rows
        acts = lax.dynamic_slice_in_dim(acts[layer], start, rows, axis=1)
        return jnp.einsum("tr,tc->rc", acts, out_grads[layer], preferred_element_type=jnp.float32)

    def block(acts, layer, step):
        which = lax.rem(chip - ways[layer] * (1 + step) + 2 * chips, chips)
        if cores == 1:
            return product(acts, layer, which, core)
        other = lax.ppermute(pack(product(acts, layer, which, 1 - core)), "dp", swap)
        return product(acts, layer, which, core) + unpack(other)

    values = [block(activations, layer, 0) for layer in range(layers)]
    if chips > 1:
        first = [pack(value) for value in values]
        activations, first = lax.optimization_barrier((activations, first))
        later = [
            [block(activations, layer, step) for layer in range(layers)]
            for step in range(1, chips)
        ]
        running = [lax.ppermute(first[i], "dp", rings[i]) for i in range(layers)]
        for step, blocks in enumerate(later, 1):
            values = [blocks[i] + unpack(running[i]) for i in range(layers)]
            if step < chips - 1:
                running = [lax.ppermute(pack(values[i]), "dp", rings[i]) for i in range(layers)]
    return values


def adam_update(grad_own, master, first_moment, second_moment, clip_factor):
    clipped = clip_factor * grad_own
    new_first = beta_first * first_moment + (1.0 - beta_first) * clipped
    new_second = beta_second * second_moment + (1.0 - beta_second) * clipped * clipped
    step_dir = new_first / first_fix / (jnp.sqrt(new_second / second_fix) + epsilon)
    new_master = master - learn_rate * (step_dir + decay_rate * master)
    return (new_master, new_first, new_second)


def on_device(activations, out_grads, master, first_moment, second_moment):
    own_rows = master.shape[0]
    layer_grads = reduce_rows(activations, out_grads)
    sum_squares, _ = device_total(sum(jnp.sum(g * g) for g in layer_grads))
    entries = (
        own_rows * lax.axis_size("tp") * lax.axis_size("dp") * master.shape[1] * master.shape[2]
    )
    limit = limit_scale * math.sqrt(entries)
    clip_factor = limit / jnp.maximum(jnp.sqrt(sum_squares), limit)
    grad_own = with_layout_constraint(jnp.stack(layer_grads, axis=1), Layout((0, 1, 2)))
    states = (grad_own, master, first_moment, second_moment)
    cut = own_rows // 2
    head = adam_update(*(x[:cut] for x in states), clip_factor)[0].astype(jnp.bfloat16)
    clip_factor, head = lax.optimization_barrier((clip_factor, head))
    head_rows = lax.all_gather(head, "dp", axis=0)
    new_master, new_first, new_second = adam_update(*states, clip_factor)
    tail = new_master[cut:].astype(jnp.bfloat16)
    tail_rows = lax.all_gather(tail, "dp", axis=0)
    tp_rows = jnp.zeros((lax.axis_size("dp"),) + master.shape, jnp.bfloat16)
    tp_rows = lax.dynamic_update_slice_in_dim(tp_rows, head_rows, 0, 1)
    tp_rows = lax.optimization_barrier(tp_rows)
    tp_rows = lax.dynamic_update_slice_in_dim(tp_rows, tail_rows, cut, 1)
    return (new_master, new_first, new_second, tp_rows.reshape((-1,) + master.shape[1:]))


def solution(mesh):
    return jax.shard_map(
        on_device,
        mesh=mesh,
        in_specs=(
            P(None, "dp", "tp"),
            P(None, "dp", None),
            P(("tp", "dp"), None, None),
            P(("tp", "dp"), None, None),
            P(("tp", "dp"), None, None),
        ),
        out_specs=(
            P(("tp", "dp"), None, None),
            P(("tp", "dp"), None, None),
            P(("tp", "dp"), None, None),
            P("tp", None, None),
        ),
        check_vma=False,
    )
```

profile of v0, /device:TPU:0, one launch (start us, length us, event | category | flops | bytes accessed | tf_op | source)
XLA Modules:
  0.0 425.0 jit_solution(9370648488881770730)
XLA Ops:
  7.2 5.8 %multiply_reduce_fusion.1 = f32[2,2048]{1,0:T(2,128)S(1)} fusion(bf16[2,1024,2048]{2,1,0:T(8,128)(2,1)} %param.5), kind=kLoop, calls=%fused_computation.1 | loop fusion | flops 12578816 | bytes 8404992 | tf_op jit(solution)/shard_map/reduce_sum | solution.py:92
  13.0 4.2 fusion.243
  17.2 0.6 reduce_max.18
  18.5 5.6 %multiply_reduce_fusion = f32[2,2048]{1,0:T(2,128)S(1)} fusion(bf16[2,1024,2048]{2,1,0:T(8,128)(2,1)} %param.6), kind=kLoop, calls=%fused_computation | loop fusion | flops 12578816 | bytes 8404992 | tf_op jit(solution)/shard_map/reduce_sum | solution.py:92
  24.1 0.6 reduce_max.19
  25.4 0.6 broadcast_in_dim.7.value_ref
  26.0 13.1 %device_total.2 = f32[2,8,128]{2,1,0:T(8,128)} custom-call(f32[8,128]{1,0:T(8,128)} %broadcast_in_dim.7.value_ref), custom_call_target="tpu_custom_call" | custom-call | tf_op jit(solution)/shard_map/device_total/pallas_call | solution.py:66
  39.1 1.2 slice.29
  41.0 3.7 fusion.74
  44.7 0.2 collective-permute-start
  44.9 4.7 %fusion.77 = f16[256,2048]{1,0:T(8,128)(2,1)} fusion(f32[]{:T(128)} %bitcast.3, bf16[2,1024,2048]{2,1,0:T(8,128)(2,1)} %param.6, bf16[1,1024,2048]{2,1,0:T(8,128)(2,1)} %get-tuple-element.21, s32[]{:T(128)S(6)} %select_n.57), kind=kOutput, calls=%fused_computation.94 | convolution fusion | flops 1075838976 | bytes 5767684 | tf_op jit(solution)/shard_map/tr,tc->rc/dot_general | solution.py:114
  49.6 0.4 collective-permute-start.1
  50.0 5.1 %fusion.160 = f16[256,2048]{1,0:T(8,128)(2,1)S(1)} fusion(f16[256,2048]{1,0:T(8,128)(2,1)S(1)} %collective-permute-done, f32[]{:T(128)} %bitcast.4, f32[]{:T(128)} %bitcast.3, bf16[2,1024,2048]{2,1,0:T(8,128)(2,1)} %param.6, bf16[1,1024,2048]{2,1,0:T(8,128)(2,1)} %get-tuple-element.22, s32[]{:T(128)S(6)} %select_n.54), kind=kOutput, calls=%fused_computation.163 | convolution fusion | flops 1078984704 | bytes 6816772 | tf_op jit(solution)/shard_map/tr,tc->rc/dot_general | solution.py:114
  55.1 5.1 %fusion.161 = f16[256,2048]{1,0:T(8,128)(2,1)S(1)} fusion(f16[256,2048]{1,0:T(8,128)(2,1)S(1)} %collective-permute-done.1, f32[]{:T(128)} %bitcast.4, f32[]{:T(128)} %bitcast.3, bf16[2,1024,2048]{2,1,0:T(8,128)(2,1)} %param.6, bf16[1,1024,2048]{2,1,0:T(8,128)(2,1)} %get-tuple-element.21, s32[]{:T(128)S(6)} %select_n.56), kind=kOutput, calls=%fused_computation.164 | convolution fusion | flops 1078984704 | bytes 6816772 | tf_op jit(solution)/shard_map/tr,tc->rc/dot_general | solution.py:114
  60.2 0.7 collective-permute-start.5
  60.9 3.1 collective-permute-start.11
  64.1 1.3 fusion.242
  65.5 1.4 fusion.86
  66.8 1.4 fusion.83
  68.2 1.4 fusion.95
  69.6 1.4 fusion.89
  71.0 0.1 collective-permute-start.8
  71.1 0.5 collective-permute-start.10
  71.6 0.1 collective-permute-start.4
  71.6 1.3 fusion.20
  72.9 1.3 fusion.24
  74.2 1.3 fusion.4
  75.5 1.4 fusion.92
  76.9 11.2 %collective-permute-done.5 = f16[256,2048]{1,0:T(8,128)(2,1)S(1)} collective-permute-done((f16[256,2048]{1,0:T(8,128)(2,1)S(1)}, f16[256,2048]{1,0:T(8,128)(2,1)S(1)}, u32[]{:S(2)}, u32[]{:S(2)}) %collective-permute-start.5) | collective-permute-done | bytes 1048608 | tf_op jit(solution)/shard_map/ppermute | solution.py:131
  88.1 0.5 collective-permute-start.3
  88.6 2.9 fusion.167
  91.5 16.8 %collective-permute-done.11 = f16[256,2048]{1,0:T(8,128)(2,1)S(1)} collective-permute-done((f16[256,2048]{1,0:T(8,128)(2,1)S(1)}, f16[256,2048]{1,0:T(8,128)(2,1)S(1)}, u32[]{:S(2)}, u32[]{:S(2)}) %collective-permute-start.11) | collective-permute-done | bytes 1048608 | tf_op jit(solution)/shard_map/ppermute | solution.py:131
  108.3 1.8 collective-permute-start.6
  110.1 2.9 fusion.169
  113.0 4.2 collective-permute-start.12
  117.2 1.3 fusion.8
  118.5 1.4 fusion.80
  119.9 0.1 collective-permute-start.2
  119.9 18.4 %collective-permute-done.6 = f16[256,2048]{1,0:T(8,128)(2,1)S(1)} collective-permute-done((f16[256,2048]{1,0:T(8,128)(2,1)S(1)}, f16[256,2048]{1,0:T(8,128)(2,1)S(1)}, u32[]{:S(2)}, u32[]{:S(2)}) %collective-permute-start.6) | collective-permute-done | bytes 1048608 | tf_op jit(solution)/shard_map/ppermute | solution.py:135
  138.3 2.9 fusion.168
  141.2 0.1 collective-permute-start.7
  141.3 18.6 %collective-permute-done.12 = f16[256,2048]{1,0:T(8,128)(2,1)S(1)} collective-permute-done((f16[256,2048]{1,0:T(8,128)(2,1)S(1)}, f16[256,2048]{1,0:T(8,128)(2,1)S(1)}, u32[]{:S(2)}, u32[]{:S(2)}) %collective-permute-start.12) | collective-permute-done | bytes 1048608 | tf_op jit(solution)/shard_map/ppermute | solution.py:135
  159.9 2.9 fusion.170
  162.7 5.3 %collective-permute-start.13 = (f16[256,2048]{1,0:T(8,128)(2,1)S(1)}, f16[256,2048]{1,0:T(8,128)(2,1)S(1)}, u32[]{:S(2)}, u32[]{:S(2)}) collective-permute-start(f16[256,2048]{1,0:T(8,128)(2,1)S(1)} %fusion.170), channel_id=1, source_target_pairs={{0,6},{1,7},{2,0},{3,1},{4,2},{5,3},{6,4},{7,5},{8,14},{9,15},{10,... | collective-permute-start | bytes 3145736 | tf_op jit(solution)/shard_map/ppermute | solution.py:135
  168.0 1.3 fusion.28
  169.3 1.3 fusion.12
  170.6 18.1 %collective-permute-done.7 = f16[256,2048]{1,0:T(8,128)(2,1)S(1)} collective-permute-done((f16[256,2048]{1,0:T(8,128)(2,1)S(1)}, f16[256,2048]{1,0:T(8,128)(2,1)S(1)}, u32[]{:S(2)}, u32[]{:S(2)}) %collective-permute-start.7) | collective-permute-done | bytes 1048608 | tf_op jit(solution)/shard_map/ppermute | solution.py:135
  188.8 3.3 multiply_reduce_fusion.3
  192.1 2.2 copy.14
  194.2 15.4 %collective-permute-done.13 = f16[256,2048]{1,0:T(8,128)(2,1)S(1)} collective-permute-done((f16[256,2048]{1,0:T(8,128)(2,1)S(1)}, f16[256,2048]{1,0:T(8,128)(2,1)S(1)}, u32[]{:S(2)}, u32[]{:S(2)}) %collective-permute-start.13) | collective-permute-done | bytes 1048608 | tf_op jit(solution)/shard_map/ppermute | solution.py:135
  209.6 3.3 multiply_reduce_fusion.2
  212.9 2.8 stack.10
  217.0 0.6 broadcast_in_dim.8.value_ref
  217.6 15.4 %device_total.3 = f32[2,8,128]{2,1,0:T(8,128)} custom-call(f32[8,128]{1,0:T(8,128)} %broadcast_in_dim.8.value_ref), custom_call_target="tpu_custom_call" | custom-call | tf_op jit(solution)/shard_map/device_total/pallas_call | solution.py:66
  233.0 1.2 slice.34
  234.9 10.6 %subtract_convert_fusion = bf16[128,2,2048]{2,1,0:T(2,128)(2,1)} fusion(f32[256,2,2048]{2,1,0:T(2,128)} %param.9, f32[256,1,2048]{2,1,0:T(1,128)} %stack.10, f32[256,1,2048]{2,1,0:T(1,128)S(1)} %copy.14, f32[256,2,2048]{2,1,0:T(2,128)} %param.8, f32[256,2,2048]{2,1,0:T(2,128)} %param.7, f32[]{:T(128)} %bitcast.20), kind=kLoop, calls=%fused_computation.171 | loop fusion | flops 9437184 | bytes 11534340 | tf_op jit(solution)/shard_map/convert_element_type | solution.py:160
  245.5 0.0 all-gather.7.cloned.1.call-start
  245.6 19.7 %multiply_subtract_fusion = (f32[256,2,2048]{2,1,0:T(2,128)S(1)}, f32[256,2,2048]{2,1,0:T(2,128)}, f32[256,2,2048]{2,1,0:T(2,128)}) fusion(f32[256,2,2048]{2,1,0:T(2,128)} %param.7, f32[256,1,2048]{2,1,0:T(1,128)} %stack.10, f32[256,1,2048]{2,1,0:T(1,128)S(1)} %copy.14, f32[]{:T(128)} %bitcast.20, f32[256,2,2048]{2,1,0:T(2,128)} %param.8, ...), kind=kLoop, calls=%fused_computation.40 | loop fusion | flops 17825792 | bytes 29360132 | tf_op jit(solution)/shard_map/sub | solution.py:144
  265.3 2.0 copy-done.1
  267.3 1.9 slice.166
  269.2 58.6 %all-gather.5.cloned.1.call-done = bf16[1024,2,2048]{2,1,0:T(2,128)(2,1)} async-done(((bf16[128,2,2048]{2,1,0:T(2,128)(2,1)}), bf16[1024,2,2048]{2,1,0:T(2,128)(2,1)}) %all-gather.5.cloned.1.call-update) | async-done | bytes 8388624 | tf_op jit(solution)/shard_map/all_gather | solution.py:162
  327.8 13.2 %dynamic_update_slice.6 = bf16[8,256,2,2048]{3,2,1,0:T(2,128)(2,1)} pad(bf16[8,128,2,2048]{3,2,1,0:T(2,128)(2,1)} %bitcast.147, bf16[]{:T(256)} %constant.139.clone.1), padding=0_0x0_128x0_0x0_0 | pad | bytes 25165826 | tf_op jit(solution)/shard_map/dynamic_update_slice | solution.py:167
  341.0 69.0 %all-gather.7.cloned.1.call-done = bf16[1024,2,2048]{2,1,0:T(2,128)(2,1)} async-done(((bf16[128,2,2048]{2,1,0:T(2,128)(2,1)}), bf16[1024,2,2048]{2,1,0:T(2,128)(2,1)}) %all-gather.7.cloned.1.call-update) | async-done | bytes 8388624 | tf_op jit(solution)/shard_map/all_gather | solution.py:165
  410.0 8.0 %constant_dynamic-update-slice_fusion = bf16[8,256,2,2048]{3,2,1,0:T(2,128)(2,1)} fusion(bf16[8,256,2,2048]{3,2,1,0:T(2,128)(2,1)} %dynamic_update_slice.6, bf16[8,128,2,2048]{3,2,1,0:T(2,128)(2,1)} %bitcast.148), kind=kLoop, calls=%fused_computation.226 | loop fusion | bytes 16777216 | tf_op jit(solution)/shard_map/dynamic_update_slice | solution.py:169
  (25 shorter events, 0.1 us)
Async XLA Ops:
  7.2 320.7 %all-gather.5.cloned.1.call-start = ((), (), s32[]{:S(2)}) async-start(), calls=%async_computation | async-start | bytes 9437184 | tf_op jit(solution)/shard_map/all_gather | solution.py:162
  7.2 5.8 %copy-start = (bf16[2,1024,2048]{2,1,0:T(8,128)(2,1)S(1)}, bf16[2,1024,2048]{2,1,0:T(8,128)(2,1)}, u32[]{:S(2)}) copy-start(bf16[2,1024,2048]{2,1,0:T(8,128)(2,1)} %param.5) | copy-start | bytes 25165828
  44.7 5.3 %collective-permute-start = (f16[256,2048]{1,0:T(8,128)(2,1)S(1)}, f16[256,2048]{1,0:T(8,128)(2,1)S(1)}, u32[]{:S(2)}, u32[]{:S(2)}) collective-permute-start(f16[256,2048]{1,0:T(8,128)(2,1)S(1)} %fusion.74), channel_id=1, source_target_pairs={{0,1},{1,0},{2,3},{3,2},{4,5},{5,4},{6,7},{7,6},{8,9},{9,8},{10,11... | collective-permute-start | bytes 3145736 | tf_op jit(solution)/shard_map/ppermute | solution.py:120
  49.6 5.5 %collective-permute-start.1 = (f16[256,2048]{1,0:T(8,128)(2,1)}, f16[256,2048]{1,0:T(8,128)(2,1)S(1)}, u32[]{:S(2)}, u32[]{:S(2)}) collective-permute-start(f16[256,2048]{1,0:T(8,128)(2,1)} %fusion.77), channel_id=1, source_target_pairs={{0,1},{1,0},{2,3},{3,2},{4,5},{5,4},{6,7},{7,6},{8,9},{9,8},{10,11... | collective-permute-start | bytes 3145736 | tf_op jit(solution)/shard_map/ppermute | solution.py:120
  50.0 14.1 %slice-start = ((s8[8388608]{0:T(1024)(128)(4,1)}), s8[4194304]{0:T(1024)(128)(4,1)S(1)}, s32[]{:S(2)}) async-start(s8[8388608]{0:T(1024)(128)(4,1)} %bitcast.142), calls=%async_computation.2 | async-start | bytes 8388608
  55.0 9.0 %slice-start.1 = ((s8[8388608]{0:T(1024)(128)(4,1)}), s8[4194304]{0:T(1024)(128)(4,1)S(1)}, s32[]{:S(2)}) async-start(s8[8388608]{0:T(1024)(128)(4,1)} %bitcast.142), calls=%async_computation.3 | async-start | bytes 8388608
  55.1 10.4 %slice-start.2 = ((s8[8388608]{0:T(1024)(128)(4,1)}), s8[4194304]{0:T(1024)(128)(4,1)S(1)}, s32[]{:S(2)}) async-start(s8[8388608]{0:T(1024)(128)(4,1)} %bitcast.145), calls=%async_computation.4 | async-start | bytes 8388608
  60.2 5.3 %slice-start.3 = ((s8[8388608]{0:T(1024)(128)(4,1)}), s8[4194304]{0:T(1024)(128)(4,1)S(1)}, s32[]{:S(2)}) async-start(s8[8388608]{0:T(1024)(128)(4,1)} %bitcast.145), calls=%async_computation.5 | async-start | bytes 8388608
  60.2 27.9 %collective-permute-start.5 = (f16[256,2048]{1,0:T(8,128)(2,1)S(1)}, f16[256,2048]{1,0:T(8,128)(2,1)S(1)}, u32[]{:S(2)}, u32[]{:S(2)}) collective-permute-start(f16[256,2048]{1,0:T(8,128)(2,1)S(1)} %fusion.160), channel_id=1, source_target_pairs={{0,2},{1,3},{2,4},{3,5},{4,6},{5,7},{6,0},{7,1},{8,10},{9,11},{10,... | collective-permute-start | bytes 3145736 | tf_op jit(solution)/shard_map/ppermute | solution.py:131
  60.9 47.4 %collective-permute-start.11 = (f16[256,2048]{1,0:T(8,128)(2,1)S(1)}, f16[256,2048]{1,0:T(8,128)(2,1)S(1)}, u32[]{:S(2)}, u32[]{:S(2)}) collective-permute-start(f16[256,2048]{1,0:T(8,128)(2,1)S(1)} %fusion.161), channel_id=1, source_target_pairs={{0,6},{1,7},{2,0},{3,1},{4,2},{5,3},{6,4},{7,5},{8,14},{9,15},{10,... | collective-permute-start | bytes 3145736 | tf_op jit(solution)/shard_map/ppermute | solution.py:131
  71.0 123.2 %collective-permute-start.8 = (f16[256,2048]{1,0:T(8,128)(2,1)S(1)}, f16[256,2048]{1,0:T(8,128)(2,1)S(1)}, u32[]{:S(2)}, u32[]{:S(2)}) collective-permute-start(f16[256,2048]{1,0:T(8,128)(2,1)S(1)} %fusion.89), channel_id=1, source_target_pairs={{0,1},{1,0},{2,3},{3,2},{4,5},{5,4},{6,7},{7,6},{8,9},{9,8},{10,11... | collective-permute-start | bytes 3145736 | tf_op jit(solution)/shard_map/ppermute | solution.py:120
  71.1 39.0 %collective-permute-start.10 = (f16[256,2048]{1,0:T(8,128)(2,1)S(1)}, f16[256,2048]{1,0:T(8,128)(2,1)S(1)}, u32[]{:S(2)}, u32[]{:S(2)}) collective-permute-start(f16[256,2048]{1,0:T(8,128)(2,1)S(1)} %fusion.95), channel_id=1, source_target_pairs={{0,1},{1,0},{2,3},{3,2},{4,5},{5,4},{6,7},{7,6},{8,9},{9,8},{10,11... | collective-permute-start | bytes 3145736 | tf_op jit(solution)/shard_map/ppermute | solution.py:120
  71.6 16.6 %collective-permute-start.4 = (f16[256,2048]{1,0:T(8,128)(2,1)S(1)}, f16[256,2048]{1,0:T(8,128)(2,1)S(1)}, u32[]{:S(2)}, u32[]{:S(2)}) collective-permute-start(f16[256,2048]{1,0:T(8,128)(2,1)S(1)} %fusion.86), channel_id=1, source_target_pairs={{0,1},{1,0},{2,3},{3,2},{4,5},{5,4},{6,7},{7,6},{8,9},{9,8},{10,11... | collective-permute-start | bytes 3145736 | tf_op jit(solution)/shard_map/ppermute | solution.py:120
  88.1 53.1 %collective-permute-start.9 = (f16[256,2048]{1,0:T(8,128)(2,1)S(1)}, f16[256,2048]{1,0:T(8,128)(2,1)S(1)}, u32[]{:S(2)}, u32[]{:S(2)}) collective-permute-start(f16[256,2048]{1,0:T(8,128)(2,1)S(1)} %fusion.92), channel_id=1, source_target_pairs={{0,1},{1,0},{2,3},{3,2},{4,5},{5,4},{6,7},{7,6},{8,9},{9,8},{10,11... | collective-permute-start | bytes 3145736 | tf_op jit(solution)/shard_map/ppermute | solution.py:120
  88.1 31.7 %collective-permute-start.3 = (f16[256,2048]{1,0:T(8,128)(2,1)S(1)}, f16[256,2048]{1,0:T(8,128)(2,1)S(1)}, u32[]{:S(2)}, u32[]{:S(2)}) collective-permute-start(f16[256,2048]{1,0:T(8,128)(2,1)S(1)} %fusion.83), channel_id=1, source_target_pairs={{0,1},{1,0},{2,3},{3,2},{4,5},{5,4},{6,7},{7,6},{8,9},{9,8},{10,11... | collective-permute-start | bytes 3145736 | tf_op jit(solution)/shard_map/ppermute | solution.py:120
  108.3 30.0 %collective-permute-start.6 = (f16[256,2048]{1,0:T(8,128)(2,1)S(1)}, f16[256,2048]{1,0:T(8,128)(2,1)S(1)}, u32[]{:S(2)}, u32[]{:S(2)}) collective-permute-start(f16[256,2048]{1,0:T(8,128)(2,1)S(1)} %fusion.167), channel_id=1, source_target_pairs={{0,2},{1,3},{2,4},{3,5},{4,6},{5,7},{6,0},{7,1},{8,10},{9,11},{10,... | collective-permute-start | bytes 3145736 | tf_op jit(solution)/shard_map/ppermute | solution.py:135
  113.0 46.9 %collective-permute-start.12 = (f16[256,2048]{1,0:T(8,128)(2,1)S(1)}, f16[256,2048]{1,0:T(8,128)(2,1)S(1)}, u32[]{:S(2)}, u32[]{:S(2)}) collective-permute-start(f16[256,2048]{1,0:T(8,128)(2,1)S(1)} %fusion.169), channel_id=1, source_target_pairs={{0,6},{1,7},{2,0},{3,1},{4,2},{5,3},{6,4},{7,5},{8,14},{9,15},{10,... | collective-permute-start | bytes 3145736 | tf_op jit(solution)/shard_map/ppermute | solution.py:135
  119.9 50.8 %collective-permute-start.2 = (f16[256,2048]{1,0:T(8,128)(2,1)S(1)}, f16[256,2048]{1,0:T(8,128)(2,1)S(1)}, u32[]{:S(2)}, u32[]{:S(2)}) collective-permute-start(f16[256,2048]{1,0:T(8,128)(2,1)S(1)} %fusion.80), channel_id=1, source_target_pairs={{0,1},{1,0},{2,3},{3,2},{4,5},{5,4},{6,7},{7,6},{8,9},{9,8},{10,11... | collective-permute-start | bytes 3145736 | tf_op jit(solution)/shard_map/ppermute | solution.py:120
  141.2 47.6 %collective-permute-start.7 = (f16[256,2048]{1,0:T(8,128)(2,1)S(1)}, f16[256,2048]{1,0:T(8,128)(2,1)S(1)}, u32[]{:S(2)}, u32[]{:S(2)}) collective-permute-start(f16[256,2048]{1,0:T(8,128)(2,1)S(1)} %fusion.168), channel_id=1, source_target_pairs={{0,2},{1,3},{2,4},{3,5},{4,6},{5,7},{6,0},{7,1},{8,10},{9,11},{10,... | collective-permute-start | bytes 3145736 | tf_op jit(solution)/shard_map/ppermute | solution.py:135
  162.7 46.9 %collective-permute-start.13 = (f16[256,2048]{1,0:T(8,128)(2,1)S(1)}, f16[256,2048]{1,0:T(8,128)(2,1)S(1)}, u32[]{:S(2)}, u32[]{:S(2)}) collective-permute-start(f16[256,2048]{1,0:T(8,128)(2,1)S(1)} %fusion.170), channel_id=1, source_target_pairs={{0,6},{1,7},{2,0},{3,1},{4,2},{5,3},{6,4},{7,5},{8,14},{9,15},{10,... | collective-permute-start | bytes 3145736 | tf_op jit(solution)/shard_map/ppermute | solution.py:135
  245.5 164.5 %all-gather.7.cloned.1.call-start = ((), (), s32[]{:S(2)}) async-start(), calls=%async_computation.1 | async-start | bytes 9437184 | tf_op jit(solution)/shard_map/all_gather | solution.py:165
  265.3 2.0 copy-start.1
Sparse Core Ops, SparseCore 0:
  245.6 82.1 all-gather.4
  329.4 80.5 all-gather.6
where the time goes:
time: 428 us; the launch traced here: 425 us
  waiting for transfers between devices  226 us (53%)
  other arithmetic  61 us (14%)
  local copies, waits for them, and re-layouts  39.2 us (9%)
  matrix products  34.5 us (8%)
  Pallas kernels  28.5 us (7%)
  between operations  18.6 us (4%)
  starting transfers between devices  17.1 us (4%)
    ppermute x4, waiting for transfers between devices, reduce_rows(): lax.ppermute(pack(values[i]), 'dp', rings[i])  70.5 us
    all_gather x1, waiting for transfers between devices, on_device(): tail_rows = lax.all_gather(tail, 'dp', axis=0)  69 us
    all_gather x1, waiting for transfers between devices, on_device(): head_rows = lax.all_gather(head, 'dp', axis=0)  58.6 us
    dot_general x16, matrix products, product(): jnp.einsum('tr,tc->rc', acts, out_grads[layer], preferred_element_type=jn...  34.5 us
    pallas_call x2, Pallas kernels, device_total(): pl.pallas_call(functools.partial(total_kernel, n_tp, n_dp), out_shape=jax...  28.5 us
    ppermute x2, waiting for transfers between devices, reduce_rows(): running = [lax.ppermute(first[i], 'dp', rings[i]) for i in range(layers)]  28 us
    sub x1, other arithmetic, adam_update(): new_master = master - learn_rate * (step_dir + decay_rate * master)  19.7 us
    dynamic_update_slice x1, local copies, waits for them, and re-layouts, on_device(): tp_rows = lax.dynamic_update_slice_in_dim(tp_rows, head_rows, 0, 1)  13.2 us
  transfers between devices with their start and end apart: 16, of which 8 were waited for; matrix products, arithmetic and copies ran while one was open for 19% of the time, Pallas kernels for 0%

commit v1 on v0

v1 whole, which is shorter than its diff:
```python
import functools
import math

import jax
import jax.numpy as jnp
from jax import lax
from jax.experimental import pallas as pl
from jax.experimental.pallas import tpu as pltpu
from jax.sharding import PartitionSpec as P

beta_first = 0.9
beta_second = 0.95
first_fix = 1.0 - 0.9**10
second_fix = 1.0 - 0.95**10
learn_rate = 0.01
decay_rate = 0.1
epsilon = 1e-08
limit_scale = 2.0
MESH = pl.DeviceIdType.MESH
CORES = 2
LANES = 128
TILE = 16
TOP = 224.0
STATE_SLOTS = 4


def decode(code, scale):
    code = code.astype(jnp.float32)
    size = jnp.abs(code)
    root = jnp.exp(jnp.log(jnp.maximum(size, 1e-37)) * (1.0 / 16.0))
    root = jnp.where(size > 0.0, root, 0.0)
    return jnp.where(code < 0.0, -root, root) * scale


def encode(value, shrink):
    x = value * shrink
    power = x * x
    power = power * power
    power = power * power
    power = power * power
    return jnp.where(x < 0.0, -power, power).astype(jnp.bfloat16)


def step_kernel(
    d,
    acts, grads, master, first, second,
    new_master, new_first, new_second, weights,
    a_buf, b_buf, part, rx, grad, wide, state, norm,
    a_own, a_send, a_recv, b_own, b_send, b_recv,
    rs_send, rs_recv, norm_send, norm_recv, state_in, state_out,
    ag_send, ag_recv, out_local, out_send, out_recv,
):
    L, T, R, N, C, AW, WC, NB = d.L, d.T, d.R, d.N, d.C, d.AW, d.WC, d.NB
    n_tp, n_dp = d.n_tp, d.n_dp
    pieces, tiles_across, lane_tiles = L * NB, WC // LANES, N // LANES
    tiles = R // TILE * tiles_across
    stride = lane_tiles * L
    index = lax.axis_index("dp")
    chip, core = index // CORES, lax.rem(index, CORES)
    partner = {"dp": chip * CORES + 1 - core}
    me = lax.axis_index("tp") * n_dp + index
    count = n_tp * n_dp

    def column(c, k):
        start = c * CORES * R + (k * R if AW == R else 0)
        return pl.ds(pl.multiple_of(start, LANES), AW)

    def a_local(l, c):
        return pltpu.make_async_copy(
            acts.at[l, :, column(c, core)], a_buf.at[0, l, c], a_own.at[l, c]
        )

    def a_remote(l, c):
        return pltpu.make_async_remote_copy(
            acts.at[l, :, column(c, 1 - core)], a_buf.at[1, l, c],
            a_send.at[l, c], a_recv.at[l, c],
            device_id=partner, device_id_type=MESH,
        )

    def b_columns(j):
        return pl.ds(pl.multiple_of(j * WC, LANES), WC)

    def b_local(l, j):
        return pltpu.make_async_copy(
            grads.at[l, :, b_columns(j)], b_buf.at[0, l, j], b_own.at[l, j]
        )

    def b_remote(l, j):
        return pltpu.make_async_remote_copy(
            grads.at[l, :, b_columns(j)], b_buf.at[1, l, j],
            b_send.at[l, j], b_recv.at[l, j],
            device_id=partner, device_id_type=MESH,
        )

    def in_order(a_copy, b_copy):
        for l in range(L):
            a_copy(l, C - 1).start()
            a_copy(l, 0).start()
            for j in range(NB):
                b_copy(l, j).start()
            for c in range(1, C - 1):
                a_copy(l, c).start()

    in_order(a_local, b_local)

    rows_q = d.rows_q
    sources = (master, first, second)
    targets = (new_master, new_first, new_second)

    def state_load(i, q):
        slot = lax.rem(q, STATE_SLOTS)
        return pltpu.make_async_copy(
            sources[i].at[pl.ds(q * rows_q, rows_q)], state.at[i, slot], state_in.at[i, slot]
        )

    def state_store(i, q):
        slot = lax.rem(q, STATE_SLOTS)
        return pltpu.make_async_copy(
            state.at[i, slot], targets[i].at[pl.ds(q * rows_q, rows_q)], state_out.at[i, slot]
        )

    barrier = pltpu.get_barrier_semaphore()

    def device(k):
        other = lax.rem(me + k, count)
        return {"tp": other // n_dp, "dp": lax.rem(other, n_dp)}

    @pl.loop(1, count)
    def _(k):
        pl.semaphore_signal(barrier, inc=1, device_id=device(k), device_id_type=MESH)

    pl.semaphore_wait(barrier, count - 1)

    in_order(a_remote, b_remote)

    for q in range(min(STATE_SLOTS, d.PQ)):
        for i in range(3):
            state_load(i, jnp.int32(q)).start()

    def product(c, l, j):
        total = None
        for w in range(CORES):
            lhs = a_buf[w, l, c]
            if AW != R:
                lhs = jnp.where(core == 0, lhs[:, :R], lhs[:, R:])
            term = lax.dot_general(
                lhs, b_buf[w, l, j], (((0,), (0,)), ((), ())),
                preferred_element_type=jnp.float32,
            )
            total = term if total is None else total + term
        part[...] = total

    def rs_copy(way, s, p):
        to = chip + 1 if way == 0 else chip - 1
        return pltpu.make_async_remote_copy(
            rx.at[way, s, p], rx.at[way, s, p],
            rs_send.at[way, s, p], rs_recv.at[way, s, p],
            device_id={"dp": to * CORES + core}, device_id_type=MESH,
        )

    def add_received(way, s, p):
        rs_copy(way, s, p).wait_recv()
        scale = rx[way, s, p, tiles].astype(jnp.float32) * (1.0 / TOP)

        @pl.loop(0, R // TILE)
        def _(r):
            rows = pl.ds(pl.multiple_of(r * TILE, TILE), TILE)
            for t in range(tiles_across):
                lanes = pl.ds(t * LANES, LANES)
                code = rx[way, s, p, r * tiles_across + t]
                part[rows, lanes] += decode(code, scale)

    def send_on(way, s, p):
        def widest(r, top):
            rows = pl.ds(pl.multiple_of(r * TILE, TILE), TILE)
            for t in range(tiles_across):
                top = jnp.maximum(top, jnp.abs(part[rows, pl.ds(t * LANES, LANES)]))
            return top

        top = lax.fori_loop(0, R // TILE, widest, jnp.zeros((TILE, LANES), jnp.float32))
        top = jnp.maximum(top, 1e-25).astype(jnp.bfloat16)
        rx[way, s, p, tiles] = top
        shrink = TOP / top.astype(jnp.float32)

        @pl.loop(0, R // TILE)
        def _(r):
            rows = pl.ds(pl.multiple_of(r * TILE, TILE), TILE)
            for t in range(tiles_across):
                value = part[rows, pl.ds(t * LANES, LANES)]
                rx[way, s, p, r * tiles_across + t] = encode(value, shrink)

        rs_copy(way, s, p).start()

    def own_rows(r, l, j, t, half):
        start = ((r * TILE + half * 8) * lane_tiles + j * tiles_across + t) * L + l
        return pl.ds(start, 8, stride=stride)

    def keep_own(l, j):
        @pl.loop(0, R // TILE)
        def _(r):
            rows = pl.ds(pl.multiple_of(r * TILE, TILE), TILE)
            for t in range(tiles_across):
                value = part[rows, pl.ds(t * LANES, LANES)]
                for half in range(2):
                    grad[own_rows(r, l, j, t, half), :] = value[half * 8 : half * 8 + 8]

    def add_own(way, s, p, l, j):
        rs_copy(way, s, p).wait_recv()
        scale = rx[way, s, p, tiles].astype(jnp.float32) * (1.0 / TOP)

        @pl.loop(0, R // TILE)
        def _(r):
            for t in range(tiles_across):
                value = decode(rx[way, s, p, r * tiles_across + t], scale)
                for half in range(2):
                    where = own_rows(r, l, j, t, half)
                    grad[where, :] = grad[where, :] + value[half * 8 : half * 8 + 8]

    @pl.loop(0, C)
    def _(s):
        high, low = C - 1 - s, s

        @pl.loop(0, pieces)
        def _(p):
            l, j = p // NB, lax.rem(p, NB)

            @pl.when(s == 0)
            def _():
                @pl.when(j == 0)
                def _():
                    for c in sorted({0, C - 1}):
                        a_local(l, c).wait()
                        a_remote(l, c).wait_recv()

                b_local(l, j).wait()
                b_remote(l, j).wait_recv()

            @pl.when((s < C - 1) & (chip < high))
            def _():
                product(high, l, j)

                @pl.when(chip > 0)
                def _():
                    add_received(0, s, p)

                send_on(0, s, p)

            @pl.when((s < C - 1) & (chip > low))
            def _():
                product(low, l, j)

                @pl.when(chip < C - 1)
                def _():
                    add_received(1, s, p)

                send_on(1, s, p)

            @pl.when(s == 0)
            def _():
                @pl.when(j == 0)
                def _():
                    for c in range(1, C - 1):
                        a_local(l, c).wait()
                        a_remote(l, c).wait_recv()

                product(chip, l, j)
                keep_own(l, j)

            @pl.when((s > 0) & (chip == C - s) & (chip > 0))
            def _():
                add_own(0, s - 1, p, l, j)

            @pl.when((s > 0) & (chip == s - 1) & (chip < C - 1))
            def _():
                add_own(1, s - 1, p, l, j)

    own_total = R * stride
    block = 64

    def square(b, sums):
        x = grad[pl.ds(pl.multiple_of(b * block, block), block), :]
        x = x * x
        for i in range(block // 8):
            sums = sums + x[i * 8 : i * 8 + 8]
        return sums

    sums = lax.fori_loop(0, own_total // block, square, jnp.zeros((8, LANES), jnp.float32))
    norm[me] = jnp.sum(sums, axis=0, keepdims=True)

    def norm_copy(k, slot):
        return pltpu.make_async_remote_copy(
            norm.at[slot], norm.at[slot], norm_send.at[k], norm_recv.at[k],
            device_id=device(k), device_id_type=MESH,
        )

    @pl.loop(1, count)
    def _(k):
        norm_copy(k, me).start()

    @pl.loop(1, count)
    def _(k):
        norm_copy(k, lax.rem(me - k + count, count)).wait_recv()

    total = jnp.sum(jnp.sum(norm[...], axis=0), axis=1, keepdims=True)
    limit = limit_scale * math.sqrt(own_total * LANES * count)
    clip = limit / jnp.maximum(jnp.sqrt(total), limit)
    clip = jnp.broadcast_to(clip, (block, LANES))

    def place(c, q):
        start = (c * CORES + core) * own_total + q * rows_q
        return pl.ds(pl.multiple_of(start, TILE), rows_q)

    def ag_copy(way, c, q):
        to = chip + 1 if way == 0 else chip - 1
        return pltpu.make_async_remote_copy(
            wide.at[c, q], wide.at[c, q], ag_send.at[way, c, q], ag_recv.at[c, q],
            device_id={"dp": to * CORES + core}, device_id_type=MESH,
        )

    def local_copy(c, q):
        return pltpu.make_async_copy(wide.at[c, q], weights.at[place(c, q)], out_local.at[c, q])

    def partner_copy(c, q):
        return pltpu.make_async_remote_copy(
            wide.at[c, q], weights.at[place(c, q)], out_send.at[c, q], out_recv.at[c, q],
            device_id=partner, device_id_type=MESH,
        )

    def partner_place(c, q):
        start = (c * CORES + 1 - core) * own_total + q * rows_q
        return pl.ds(pl.multiple_of(start, TILE), rows_q)

    def partner_arrival(c, q):
        return pltpu.make_async_remote_copy(
            wide.at[c, q], weights.at[partner_place(c, q)], out_send.at[c, q], out_recv.at[c, q],
            device_id=partner, device_id_type=MESH,
        )

    @pl.loop(0, d.PQ)
    def _(q):
        slot = lax.rem(q, STATE_SLOTS)
        for i in range(3):
            state_load(i, q).wait()

        @pl.loop(0, rows_q // block)
        def _(b):
            here = pl.ds(pl.multiple_of(b * block, block), block)
            there = pl.ds(pl.multiple_of(q * rows_q + b * block, block), block)
            clipped = clip * grad[there, :]
            moment = beta_first * state[1, slot, here, :] + (1.0 - beta_first) * clipped
            spread = beta_second * state[2, slot, here, :]
            spread = spread + (1.0 - beta_second) * clipped * clipped
            old = state[0, slot, here, :]
            direction = moment / first_fix / (jnp.sqrt(spread / second_fix) + epsilon)
            new = old - learn_rate * (direction + decay_rate * old)
            state[0, slot, here, :] = new
            state[1, slot, here, :] = moment
            state[2, slot, here, :] = spread
            wide[chip, q, here, :] = new.astype(jnp.bfloat16)

        @pl.when(chip > 0)
        def _():
            ag_copy(1, chip, q).start()

        @pl.when(chip < C - 1)
        def _():
            ag_copy(0, chip, q).start()

        for i in range(3):
            state_store(i, q).start()
        local_copy(chip, q).start()
        partner_copy(chip, q).start()

        @pl.when((q > 0) & (q - 1 + STATE_SLOTS < d.PQ))
        def _():
            for i in range(3):
                state_store(i, q - 1).wait()
                state_load(i, q - 1 + STATE_SLOTS).start()

    @pl.loop(1, C)
    def _(far):
        @pl.loop(0, d.PQ)
        def _(q):
            @pl.when(chip - far >= 0)
            def _():
                ag_copy(0, chip - far, q).wait_recv()

                @pl.when(chip < C - 1)
                def _():
                    ag_copy(0, chip - far, q).start()

                local_copy(chip - far, q).start()
                partner_copy(chip - far, q).start()

            @pl.when(chip + far < C)
            def _():
                ag_copy(1, chip + far, q).wait_recv()

                @pl.when(chip > 0)
                def _():
                    ag_copy(1, chip + far, q).start()

                local_copy(chip + far, q).start()
                partner_copy(chip + far, q).start()

    for q in range(max(0, d.PQ - STATE_SLOTS), d.PQ):
        for i in range(3):
            state_store(i, jnp.int32(q)).wait()

    for l in range(L):
        for c in range(C):
            a_remote(l, c).wait_send()
        for j in range(NB):
            b_remote(l, j).wait_send()

    @pl.loop(1, count)
    def _(k):
        norm_copy(k, me).wait_send()

    @pl.loop(0, C - 1)
    def _(s):
        @pl.loop(0, pieces)
        def _(p):
            @pl.when(chip < C - 1 - s)
            def _():
                rs_copy(0, s, p).wait_send()

            @pl.when(chip > s)
            def _():
                rs_copy(1, s, p).wait_send()

    @pl.loop(0, C)
    def _(c):
        @pl.loop(0, d.PQ)
        def _(q):
            @pl.when((c <= chip) & (chip < C - 1))
            def _():
                ag_copy(0, c, q).wait_send()

            @pl.when((c >= chip) & (chip > 0))
            def _():
                ag_copy(1, c, q).wait_send()

            local_copy(c, q).wait()
            partner_copy(c, q).wait_send()
            partner_arrival(c, q).wait_recv()


class Sizes:
    pass


def whole_step(acts, grads, master, first, second):
    d = Sizes()
    d.L, d.T, width = acts.shape
    d.N = grads.shape[2]
    d.n_tp, d.n_dp = lax.axis_size("tp"), lax.axis_size("dp")
    d.C = d.n_dp // CORES
    d.R = width // d.n_dp
    d.AW = d.R if d.R % LANES == 0 else CORES * d.R
    d.WC = math.gcd(512, d.N)
    d.NB = d.N // d.WC
    d.PQ = 8
    pieces = d.L * d.NB
    tiles = d.R // TILE * (d.WC // LANES)
    rows = d.R * d.L * d.N // LANES
    d.rows_q = rows // d.PQ
    count = d.n_tp * d.n_dp
    hbm = pl.BlockSpec(memory_space=pl.ANY)
    dma = pltpu.SemaphoreType.DMA
    flat = jax.ShapeDtypeStruct((rows, LANES), jnp.float32)
    return pl.pallas_call(
        functools.partial(step_kernel, d),
        out_shape=(flat, flat, flat, jax.ShapeDtypeStruct((d.n_dp * rows, LANES), jnp.bfloat16)),
        in_specs=[hbm] * 5,
        out_specs=[hbm] * 4,
        scratch_shapes=[
            pltpu.VMEM((CORES, d.L, d.C, d.T, d.AW), jnp.bfloat16),
            pltpu.VMEM((CORES, d.L, d.NB, d.T, d.WC), jnp.bfloat16),
            pltpu.VMEM((d.R, d.WC), jnp.float32),
            pltpu.VMEM((2, d.C - 1, pieces, tiles + 1, TILE, LANES), jnp.bfloat16),
            pltpu.VMEM((rows, LANES), jnp.float32),
            pltpu.VMEM((d.C, d.PQ, d.rows_q, LANES), jnp.bfloat16),
            pltpu.VMEM((3, STATE_SLOTS, d.rows_q, LANES), jnp.float32),
            pltpu.VMEM((count, 1, LANES), jnp.float32),
            dma((d.L, d.C)), dma((d.L, d.C)), dma((d.L, d.C)),
            dma((d.L, d.NB)), dma((d.L, d.NB)), dma((d.L, d.NB)),
            dma((2, d.C - 1, pieces)), dma((2, d.C - 1, pieces)),
            dma((count,)), dma((count,)),
            dma((3, STATE_SLOTS)), dma((3, STATE_SLOTS)),
            dma((2, d.C, d.PQ)), dma((d.C, d.PQ)),
            dma((d.C, d.PQ)), dma((d.C, d.PQ)), dma((d.C, d.PQ)),
        ],
        compiler_params=pltpu.CompilerParams(
            collective_id=0, has_side_effects=True, vmem_limit_bytes=67043328
        ),
        name="whole_step",
    )(acts, grads, master, first, second)


def to_rows(x):
    r, l, n = x.shape
    return x.reshape(r, l, n // LANES, LANES).transpose(0, 2, 1, 3).reshape(-1, LANES)


def from_rows(y, l, n):
    return y.reshape(-1, n // LANES, l, LANES).transpose(0, 2, 1, 3).reshape(-1, l, n)


def on_device(activations, out_grads, master, first_moment, second_moment):
    states = [to_rows(x) for x in (master, first_moment, second_moment)]
    outs = whole_step(activations, out_grads, *states)
    return tuple(from_rows(y, *master.shape[1:]) for y in outs)


def solution(mesh):
    return jax.shard_map(
        on_device,
        mesh=mesh,
        in_specs=(
            P(None, "dp", "tp"),
            P(None, "dp", None),
            P(("tp", "dp"), None, None),
            P(("tp", "dp"), None, None),
            P(("tp", "dp"), None, None),
        ),
        out_specs=(
            P(("tp", "dp"), None, None),
            P(("tp", "dp"), None, None),
            P(("tp", "dp"), None, None),
            P("tp", None, None),
        ),
        check_vma=False,
    )
```

time: 428 us -> 376 us (0.88)
  Pallas kernels: 28.5 us -> 353 us
  waiting for transfers between devices: 226 us -> 0 us
  other arithmetic: 61 us -> 0 us
  matrix products: 34.5 us -> 0 us
  between operations: 18.6 us -> 0.65 us
  starting transfers between devices: 17.1 us -> 0 us
  local copies, waits for them, and re-layouts: 39.2 us -> 22.5 us
    pallas_call x2 -> x1, Pallas kernels: 28.5 us -> 353 us  [whole_step(): pl.pallas_call(functools.partial(step_kernel, d), out_shape=(flat, flat,...]
    all_gather x2 -> x0, waiting for transfers between devices: 128 us -> none  [the longest x1 69 us: on_device(): tail_rows = lax.all_gather(tail, 'dp', axis=0)]
    ppermute x14 -> x0, waiting for transfers between devices: 98.5 us -> none  [the longest x4 70.5 us: reduce_rows(): lax.ppermute(pack(values[i]), 'dp', rings[i])]
    dot_general x16 -> x0, matrix products: 34.5 us -> none  [product(): jnp.einsum('tr,tc->rc', acts, out_grads[layer], preferred_element_type=jn...]
    convert_element_type x5 -> x0, other arithmetic: 22.1 us -> none  [the longest x4 11.5 us: pack(): return (x * jnp.abs(x)).astype(jnp.float16)]
    dynamic_update_slice x2 -> x0, local copies, waits for them, and re-layouts: 21.2 us -> none  [the longest x1 13.2 us: on_device(): tp_rows = lax.dynamic_update_slice_in_dim(tp_rows, head_rows, 0, 1)]
    unnamed x12 -> x8, local copies, waits for them, and re-layouts: 2.05 us -> 22.5 us
    sub x1 -> x0, other arithmetic: 19.7 us -> none  [adam_update(): new_master = master - learn_rate * (step_dir + decay_rate * master)]
  transfers between devices with their start and end apart: 16 -> 0, of which waited for: 8 -> 0; matrix products, arithmetic and copies ran while one was open for 19% -> 0% of each run, Pallas kernels for 0% -> 0%
where the time goes in v1:
time: 376 us
  Pallas kernels  353 us (94%)
  local copies, waits for them, and re-layouts  22.5 us (6%)
    pallas_call x1, Pallas kernels, whole_step(): pl.pallas_call(functools.partial(step_kernel, d), out_shape=(flat, flat,...  353 us
    unnamed x8, local copies, waits for them, and re-layouts  22.5 us

profile of v1, /device:TPU:0, one launch (start us, length us, event | category | flops | bytes accessed | tf_op | source)
XLA Modules:
  0.0 375.9 jit_solution(10210315593662021346)
XLA Ops:
  0.6 352.8 %whole_step.1 = (f32[8192,128]{1,0:T(8,128)}, f32[8192,128]{1,0:T(8,128)}, f32[8192,128]{1,0:T(8,128)}, bf16[65536,128]{1,0:T(8,128)(2,1)}) custom-call(bf16[2,1024,2048]{2,1,0:T(8,128)(2,1)} %acts.1, bf16[2,1024,2048]{2,1,0:T(8,128)(2,1)} %grads.1, f32[8192,128]{1,0:T(8,128)} %bitcast.36, f32[8192,128]{1,0:T(8,128)} %bitcast.37, f32[8192,128]{1,0:T(8,128)} %bitcast.38), custom_call_target="tpu_custom_call" | custom-call | tf_op jit(solution)/shard_map/whole_step/pallas_call | solution.py:472
  353.4 0.0 copy-start.1
  353.4 6.3 %copy.20 = f32[256,2,2048]{2,1,0:T(2,128)} copy(f32[256,2,2048]{2,1,0:T(2,128)} %bitcast.41) | data formatting | bytes 8388608
  359.7 0.0 copy-start
  359.7 6.5 %copy.21 = f32[256,2,2048]{2,1,0:T(2,128)} copy(f32[256,2,2048]{2,1,0:T(2,128)} %bitcast.40) | data formatting | bytes 8388608
  366.2 0.0 copy-done.1
  366.2 2.1 copy.22
  368.3 1.4 copy-done
  369.8 6.2 %copy.23 = bf16[2048,2,2048]{2,1,0:T(2,128)(2,1)} copy(bf16[2048,2,2048]{2,1,0:T(2,128)(2,1)S(1)} %bitcast.35) | data formatting | bytes 33554432
Async XLA Ops:
  353.4 12.8 %copy-start.1 = (f32[8192,128]{1,0:T(8,128)S(1)}, f32[8192,128]{1,0:T(8,128)}, u32[]{:S(2)}) copy-start(f32[8192,128]{1,0:T(8,128)} %get-tuple-element.10) | copy-start | bytes 12582916
  359.7 10.1 %copy-start = (bf16[65536,128]{1,0:T(8,128)(2,1)S(1)}, bf16[65536,128]{1,0:T(8,128)(2,1)}, u32[]{:S(2)}) copy-start(bf16[65536,128]{1,0:T(8,128)(2,1)} %get-tuple-element.11) | copy-start | bytes 50331652

commit v2 on v1

--- a/solution.py
+++ b/solution.py
@@ -22,6 +22,7 @@
 TILE = 16
 TOP = 224.0
 STATE_SLOTS = 4
+LAG = 2
 
 
 def decode(code, scale):
@@ -216,63 +217,66 @@
                     where = own_rows(r, l, j, t, half)
                     grad[where, :] = grad[where, :] + value[half * 8 : half * 8 + 8]
 
-    @pl.loop(0, C)
-    def _(s):
-        high, low = C - 1 - s, s
-
-        @pl.loop(0, pieces)
-        def _(p):
-            l, j = p // NB, lax.rem(p, NB)
-
-            @pl.when(s == 0)
-            def _():
-                @pl.when(j == 0)
-                def _():
-                    for c in sorted({0, C - 1}):
-                        a_local(l, c).wait()
-                        a_remote(l, c).wait_recv()
-
-                b_local(l, j).wait()
-                b_remote(l, j).wait_recv()
-
-            @pl.when((s < C - 1) & (chip < high))
-            def _():
-                product(high, l, j)
-
-                @pl.when(chip > 0)
-                def _():
-                    add_received(0, s, p)
-
-                send_on(0, s, p)
-
-            @pl.when((s < C - 1) & (chip > low))
-            def _():
-                product(low, l, j)
-
-                @pl.when(chip < C - 1)
-                def _():
-                    add_received(1, s, p)
-
-                send_on(1, s, p)
-
-            @pl.when(s == 0)
-            def _():
-                @pl.when(j == 0)
-                def _():
-                    for c in range(1, C - 1):
-                        a_local(l, c).wait()
-                        a_remote(l, c).wait_recv()
-
-                product(chip, l, j)
-                keep_own(l, j)
-
-            @pl.when((s > 0) & (chip == C - s) & (chip > 0))
-            def _():
-                add_own(0, s - 1, p, l, j)
-
-            @pl.when((s > 0) & (chip == s - 1) & (chip < C - 1))
-            def _():
-                add_own(1, s - 1, p, l, j)
+    steps = (C - 1) * pieces
+
+    def stream(way, t):
+        hops = chip if way == 0 else C - 1 - chip
+        n = t - LAG * hops
+        s, p = n // pieces, lax.rem(n, pieces)
+        owner = C - 1 - s if way == 0 else s
+        ahead = chip < owner if way == 0 else chip > owner
+
+        @pl.when((n >= 0) & (n < steps) & ahead)
+        def _():
+            product(owner, p // NB, lax.rem(p, NB))
+
+            @pl.when(hops > 0)
+            def _():
+                add_received(way, s, p)
+
+            send_on(way, s, p)
+
+    def arrival(way, t):
+        hops = chip if way == 0 else C - 1 - chip
+        n = t - LAG * hops - 1
+        s, p = n // pieces, lax.rem(n, pieces)
+        owner = C - 1 - s if way == 0 else s
+
+        @pl.when((n >= 0) & (n < steps) & (chip == owner) & (hops > 0))
+        def _():
+            add_own(way, s, p, p // NB, lax.rem(p, NB))
+
+    @pl.loop(0, steps + LAG * (C - 1) + 1)
+    def _(t):
+        l, j = t // NB, lax.rem(t, NB)
+
+        @pl.when(t < pieces)
+        def _():
+            @pl.when(j == 0)
+            def _():
+                for c in sorted({0, C - 1}):
+                    a_local(l, c).wait()
+                    a_remote(l, c).wait_recv()
+
+            b_local(l, j).wait()
+            b_remote(l, j).wait_recv()
+
+        stream(0, t)
+        stream(1, t)
+
+        @pl.when(t < pieces)
+        def _():
+            @pl.when(j == 0)
+            def _():
+                for c in range(1, C - 1):
+                    a_local(l, c).wait()
+                    a_remote(l, c).wait_recv()
+
+            product(chip, l, j)
+            keep_own(l, j)
+
+        arrival(0, t)
+        arrival(1, t)
 
     own_total = R * stride
     block = 64

time: 376 us -> 324 us (0.86)
  Pallas kernels: 353 us -> 301 us
    pallas_call x1, Pallas kernels: 353 us -> 301 us  [whole_step(): pl.pallas_call(functools.partial(step_kernel, d), out_shape=(flat, flat,...]
where the time goes in v2:
time: 324 us
  Pallas kernels  301 us (93%)
  local copies, waits for them, and re-layouts  22.5 us (7%)
    pallas_call x1, Pallas kernels, whole_step(): pl.pallas_call(functools.partial(step_kernel, d), out_shape=(flat, flat,...  301 us
    unnamed x8, local copies, waits for them, and re-layouts  22.5 us

profile of v2, /device:TPU:0, one launch (start us, length us, event | category | flops | bytes accessed | tf_op | source)
XLA Modules:
  0.0 324.1 jit_solution(3838452757659755740)
XLA Ops:
  0.6 300.9 %whole_step.1 = (f32[8192,128]{1,0:T(8,128)}, f32[8192,128]{1,0:T(8,128)}, f32[8192,128]{1,0:T(8,128)}, bf16[65536,128]{1,0:T(8,128)(2,1)}) custom-call(bf16[2,1024,2048]{2,1,0:T(8,128)(2,1)} %acts.1, bf16[2,1024,2048]{2,1,0:T(8,128)(2,1)} %grads.1, f32[8192,128]{1,0:T(8,128)} %bitcast.36, f32[8192,128]{1,0:T(8,128)} %bitcast.37, f32[8192,128]{1,0:T(8,128)} %bitcast.38), custom_call_target="tpu_custom_call" | custom-call | tf_op jit(solution)/shard_map/whole_step/pallas_call | solution.py:476
  301.6 0.0 copy-start.1
  301.6 6.3 %copy.20 = f32[256,2,2048]{2,1,0:T(2,128)} copy(f32[256,2,2048]{2,1,0:T(2,128)} %bitcast.41) | data formatting | bytes 8388608
  307.9 0.0 copy-start
  307.9 6.5 %copy.21 = f32[256,2,2048]{2,1,0:T(2,128)} copy(f32[256,2,2048]{2,1,0:T(2,128)} %bitcast.40) | data formatting | bytes 8388608
  314.4 0.0 copy-done.1
  314.4 2.1 copy.22
  316.5 1.4 copy-done
  317.9 6.2 %copy.23 = bf16[2048,2,2048]{2,1,0:T(2,128)(2,1)} copy(bf16[2048,2,2048]{2,1,0:T(2,128)(2,1)S(1)} %bitcast.35) | data formatting | bytes 33554432
Async XLA Ops:
  301.6 12.8 %copy-start.1 = (f32[8192,128]{1,0:T(8,128)S(1)}, f32[8192,128]{1,0:T(8,128)}, u32[]{:S(2)}) copy-start(f32[8192,128]{1,0:T(8,128)} %get-tuple-element.10) | copy-start | bytes 12582916
  307.9 10.1 %copy-start = (bf16[65536,128]{1,0:T(8,128)(2,1)S(1)}, bf16[65536,128]{1,0:T(8,128)(2,1)}, u32[]{:S(2)}) copy-start(bf16[65536,128]{1,0:T(8,128)(2,1)} %get-tuple-element.11) | copy-start | bytes 50331652

commit v3 on v2

--- a/solution.py
+++ b/solution.py
@@ -23,6 +23,9 @@
 TOP = 224.0
 STATE_SLOTS = 4
 LAG = 2
+SPLIT = 2
+BEHIND = 3
+FLIGHT = 2
 
 
 def decode(code, scale):
@@ -46,16 +49,17 @@
     d,
     acts, grads, master, first, second,
     new_master, new_first, new_second, weights,
-    a_buf, b_buf, part, rx, grad, wide, state, norm,
+    a_buf, b_buf, part, rx, tot, grad, wide, state, squares, norm,
     a_own, a_send, a_recv, b_own, b_send, b_recv,
-    rs_send, rs_recv, norm_send, norm_recv, state_in, state_out,
+    rs_send, rs_recv, tot_send, tot_recv, norm_send, norm_recv, state_in, state_out,
     ag_send, ag_recv, out_local, out_send, out_recv,
 ):
     L, T, R, N, C, AW, WC, NB = d.L, d.T, d.R, d.N, d.C, d.AW, d.WC, d.NB
     n_tp, n_dp = d.n_tp, d.n_dp
     pieces, tiles_across, lane_tiles = L * NB, WC // LANES, N // LANES
     tiles = R // TILE * tiles_across
-    stride = lane_tiles * L
+    group = tiles_across * L
+    half, rows_u = C // 2, R // SPLIT
     index = lax.axis_index("dp")
     chip, core = index // CORES, lax.rem(index, CORES)
     partner = {"dp": chip * CORES + 1 - core}
@@ -95,29 +99,38 @@
 
     def in_order(a_copy, b_copy):
         for l in range(L):
-            a_copy(l, C - 1).start()
-            a_copy(l, 0).start()
-            for j in range(NB):
+            for c in sorted({half - 1, half}):
+                a_copy(l, c).start()
+        for j in range(NB):
+            for l in range(L):
                 b_copy(l, j).start()
-            for c in range(1, C - 1):
-                a_copy(l, c).start()
+        for c in range(C):
+            if c not in (half - 1, half):
+                for l in range(L):
+                    a_copy(l, c).start()
 
     in_order(a_local, b_local)
 
-    rows_q = d.rows_q
     sources = (master, first, second)
     targets = (new_master, new_first, new_second)
+
+    def unit(start, q):
+        rows = start + lax.rem(q, SPLIT) * rows_u
+        return (
+            pl.ds(pl.multiple_of(rows, TILE), rows_u),
+            pl.ds(pl.multiple_of(q // SPLIT * group, group), group),
+        )
 
     def state_load(i, q):
         slot = lax.rem(q, STATE_SLOTS)
         return pltpu.make_async_copy(
-            sources[i].at[pl.ds(q * rows_q, rows_q)], state.at[i, slot], state_in.at[i, slot]
+            sources[i].at[unit(0, q)], state.at[i, slot], state_in.at[i, slot]
         )
 
     def state_store(i, q):
         slot = lax.rem(q, STATE_SLOTS)
         return pltpu.make_async_copy(
-            state.at[i, slot], targets[i].at[pl.ds(q * rows_q, rows_q)], state_out.at[i, slot]
+            state.at[i, slot], targets[i].at[unit(0, q)], state_out.at[i, slot]
         )
 
     barrier = pltpu.get_barrier_semaphore()
@@ -171,7 +184,7 @@
                 code = rx[way, s, p, r * tiles_across + t]
                 part[rows, lanes] += decode(code, scale)
 
-    def send_on(way, s, p):
+    def pack(way, s, p):
         def widest(r, top):
             rows = pl.ds(pl.multiple_of(r * TILE, TILE), TILE)
             for t in range(tiles_across):
@@ -190,106 +203,125 @@
                 value = part[rows, pl.ds(t * LANES, LANES)]
                 rx[way, s, p, r * tiles_across + t] = encode(value, shrink)
 
-        rs_copy(way, s, p).start()
-
-    def own_rows(r, l, j, t, half):
-        start = ((r * TILE + half * 8) * lane_tiles + j * tiles_across + t) * L + l
-        return pl.ds(start, 8, stride=stride)
-
-    def keep_own(l, j):
+    def put(r, l, j, t, value):
+        for k in range(TILE // 8):
+            start = (j * R + r * TILE + k * 8) * group + t * L + l
+            grad[pl.ds(start, 8, stride=group), :] = value[k * 8 : k * 8 + 8]
+
+    def keep_part(l, j):
         @pl.loop(0, R // TILE)
         def _(r):
             rows = pl.ds(pl.multiple_of(r * TILE, TILE), TILE)
             for t in range(tiles_across):
-                value = part[rows, pl.ds(t * LANES, LANES)]
-                for half in range(2):
-                    grad[own_rows(r, l, j, t, half), :] = value[half * 8 : half * 8 + 8]
-
-    def add_own(way, s, p, l, j):
-        rs_copy(way, s, p).wait_recv()
-        scale = rx[way, s, p, tiles].astype(jnp.float32) * (1.0 / TOP)
-
-        @pl.loop(0, R // TILE)
-        def _(r):
+                put(r, l, j, t, part[rows, pl.ds(t * LANES, LANES)])
+
+    def add_squares():
+        def square(r, sums):
+            rows = pl.ds(pl.multiple_of(r * TILE, TILE), TILE)
             for t in range(tiles_across):
-                value = decode(rx[way, s, p, r * tiles_across + t], scale)
-                for half in range(2):
-                    where = own_rows(r, l, j, t, half)
-                    grad[where, :] = grad[where, :] + value[half * 8 : half * 8 + 8]
-
-    steps = (C - 1) * pieces
+                x = part[rows, pl.ds(t * LANES, LANES)]
+                sums = sums + x * x
+            return sums
+
+        squares[...] = lax.fori_loop(0, R // TILE, square, squares[...])
+
+    def owner_of(way, s):
+        return half + s if way == 0 else half - 1 - s
+
+    def tot_copy(way, s, p):
+        return pltpu.make_async_remote_copy(
+            rx.at[way, s, p], tot.at[p], tot_send.at[s, p], tot_recv.at[p],
+            device_id={"dp": owner_of(way, s) * CORES + core}, device_id_type=MESH,
+        )
+
+    steps = half * pieces
+    squares[...] = jnp.zeros_like(squares)
 
     def stream(way, t):
         hops = chip if way == 0 else C - 1 - chip
         n = t - LAG * hops
         s, p = n // pieces, lax.rem(n, pieces)
-        owner = C - 1 - s if way == 0 else s
-        ahead = chip < owner if way == 0 else chip > owner
-
-        @pl.when((n >= 0) & (n < steps) & ahead)
-        def _():
-            product(owner, p // NB, lax.rem(p, NB))
+        l, j = lax.rem(p, L), p // L
+
+        @pl.when((n >= 0) & (n < steps))
+        def _():
+            product(owner_of(way, s), l, j)
 
             @pl.when(hops > 0)
             def _():
                 add_received(way, s, p)
 
-            send_on(way, s, p)
-
-    def arrival(way, t):
-        hops = chip if way == 0 else C - 1 - chip
-        n = t - LAG * hops - 1
-        s, p = n // pieces, lax.rem(n, pieces)
-        owner = C - 1 - s if way == 0 else s
-
-        @pl.when((n >= 0) & (n < steps) & (chip == owner) & (hops > 0))
-        def _():
-            add_own(way, s, p, p // NB, lax.rem(p, NB))
-
-    @pl.loop(0, steps + LAG * (C - 1) + 1)
+            @pl.when(hops == C - 1)
+            def _():
+                add_squares()
+
+            last = (hops == C - 1) & (s == half - 1)
+
+            @pl.when(last)
+            def _():
+                keep_part(l, j)
+
+            @pl.when(jnp.logical_not(last))
+            def _():
+                pack(way, s, p)
+
+            @pl.when((hops < C - 1) & (n >= FLIGHT))
+            def _():
+                before = n - FLIGHT
+                rs_copy(way, before // pieces, lax.rem(before, pieces)).wait_send()
+
+            @pl.when(hops < C - 1)
+            def _():
+                rs_copy(way, s, p).start()
+
+    totals = (half - 1) * pieces
+    leave = max(steps, totals + LAG * (C - 1))
+    in_loop = min(totals, steps + LAG * (C - 1) - leave)
+
+    def at_sink(way):
+        return chip == (C - 1 if way == 0 else 0)
+
+    def send_total(n):
+        for way in range(2):
+            @pl.when(at_sink(way))
+            def _():
+                @pl.when(n >= FLIGHT)
+                def _():
+                    before = n - FLIGHT
+                    tot_copy(way, before // pieces, lax.rem(before, pieces)).wait_send()
+
+                tot_copy(way, n // pieces, lax.rem(n, pieces)).start()
+
+    @pl.loop(0, steps + LAG * (C - 1))
     def _(t):
-        l, j = t // NB, lax.rem(t, NB)
+        l, j = lax.rem(t, L), t // L
 
         @pl.when(t < pieces)
         def _():
             @pl.when(j == 0)
             def _():
-                for c in sorted({0, C - 1}):
+                for c in sorted({half - 1, half}):
                     a_local(l, c).wait()
                     a_remote(l, c).wait_recv()
 
             b_local(l, j).wait()
             b_remote(l, j).wait_recv()
 
+        @pl.when((t >= pieces) & (t < pieces + L))
+        def _():
+            for c in range(C):
+                if c not in (half - 1, half):
+                    a_local(t - pieces, c).wait()
+                    a_remote(t - pieces, c).wait_recv()
+
         stream(0, t)
         stream(1, t)
 
-        @pl.when(t < pieces)
-        def _():
-            @pl.when(j == 0)
-            def _():
-                for c in range(1, C - 1):
-                    a_local(l, c).wait()
-                    a_remote(l, c).wait_recv()
-
-            product(chip, l, j)
-            keep_own(l, j)
-
-        arrival(0, t)
-        arrival(1, t)
-
-    own_total = R * stride
-    block = 64
-
-    def square(b, sums):
-        x = grad[pl.ds(pl.multiple_of(b * block, block), block), :]
-        x = x * x
-        for i in range(block // 8):
-            sums = sums + x[i * 8 : i * 8 + 8]
-        return sums
-
-    sums = lax.fori_loop(0, own_total // block, square, jnp.zeros((8, LANES), jnp.float32))
-    norm[me] = jnp.sum(sums, axis=0, keepdims=True)
+        @pl.when((t >= leave) & (t < leave + in_loop))
+        def _():
+            send_total(t - leave)
+
+    norm[me] = jnp.sum(squares[...], axis=0, keepdims=True)
 
     def norm_copy(k, slot):
         return pltpu.make_async_remote_copy(
@@ -297,22 +329,42 @@
             device_id=device(k), device_id_type=MESH,
         )
 
+    at_end = (chip == 0) | (chip == C - 1)
+
+    def from_end(k):
+        other = lax.rem(lax.rem(me - k + count, count), n_dp) // CORES
+        return (other == 0) | (other == C - 1)
+
+    @pl.when(at_end)
+    def _():
+        @pl.loop(1, count)
+        def _(k):
+            norm_copy(k, me).start()
+
     @pl.loop(1, count)
     def _(k):
-        norm_copy(k, me).start()
-
-    @pl.loop(1, count)
-    def _(k):
-        norm_copy(k, lax.rem(me - k + count, count)).wait_recv()
-
-    total = jnp.sum(jnp.sum(norm[...], axis=0), axis=1, keepdims=True)
-    limit = limit_scale * math.sqrt(own_total * LANES * count)
+        @pl.when(from_end(k))
+        def _():
+            norm_copy(k, lax.rem(me - k + count, count)).wait_recv()
+
+    @pl.loop(in_loop, totals)
+    def _(n):
+        send_total(n)
+
+    total = None
+    for a in range(n_tp):
+        for c in sorted({0, C - 1}):
+            for k in range(CORES):
+                row = norm[a * n_dp + c * CORES + k]
+                total = row if total is None else total + row
+    total = jnp.sum(total, axis=1, keepdims=True)
+    limit = limit_scale * math.sqrt(R * L * N * count)
     clip = limit / jnp.maximum(jnp.sqrt(total), limit)
-    clip = jnp.broadcast_to(clip, (block, LANES))
+    block = 8
+    clip = jnp.broadcast_to(clip, (block * group, LANES))
 
     def place(c, q):
-        start = (c * CORES + core) * own_total + q * rows_q
-        return pl.ds(pl.multiple_of(start, TILE), rows_q)
+        return unit((c * CORES + core) * R, q)
 
     def ag_copy(way, c, q):
         to = chip + 1 if way == 0 else chip - 1
@@ -331,8 +383,7 @@
         )
 
     def partner_place(c, q):
-        start = (c * CORES + 1 - core) * own_total + q * rows_q
-        return pl.ds(pl.multiple_of(start, TILE), rows_q)
+        return unit((c * CORES + 1 - core) * R, q)
 
     def partner_arrival(c, q):
         return pltpu.make_async_remote_copy(
@@ -340,27 +391,46 @@
             device_id=partner, device_id_type=MESH,
         )
 
-    @pl.loop(0, d.PQ)
-    def _(q):
-        slot = lax.rem(q, STATE_SLOTS)
+    def update(q):
+        slot, j = lax.rem(q, STATE_SLOTS), q // SPLIT
+
+        @pl.when(jnp.logical_not(at_end) & (lax.rem(q, SPLIT) == 0))
+        def _():
+            for l in range(L):
+                p = j * L + l
+                tot_copy(0, 0, p).wait_recv()
+                scale = tot[p, tiles].astype(jnp.float32) * (1.0 / TOP)
+
+                @pl.loop(0, R // TILE)
+                def _(r):
+                    for t in range(tiles_across):
+                        put(r, l, j, t, decode(tot[p, r * tiles_across + t], scale))
+
         for i in range(3):
             state_load(i, q).wait()
 
-        @pl.loop(0, rows_q // block)
+        @pl.loop(0, rows_u // block)
         def _(b):
             here = pl.ds(pl.multiple_of(b * block, block), block)
-            there = pl.ds(pl.multiple_of(q * rows_q + b * block, block), block)
+            start = (j * R + lax.rem(q, SPLIT) * rows_u + b * block) * group
+            there = pl.ds(pl.multiple_of(start, block * group), block * group)
+
+            def read(i):
+                return state[i, slot, here].reshape(block * group, LANES)
+
+            def write(i, value):
+                state[i, slot, here] = value.reshape(block, group, LANES)
+
             clipped = clip * grad[there, :]
-            moment = beta_first * state[1, slot, here, :] + (1.0 - beta_first) * clipped
-            spread = beta_second * state[2, slot, here, :]
-            spread = spread + (1.0 - beta_second) * clipped * clipped
-            old = state[0, slot, here, :]
+            moment = beta_first * read(1) + (1.0 - beta_first) * clipped
+            spread = beta_second * read(2) + (1.0 - beta_second) * clipped * clipped
+            old = read(0)
             direction = moment / first_fix / (jnp.sqrt(spread / second_fix) + epsilon)
             new = old - learn_rate * (direction + decay_rate * old)
-            state[0, slot, here, :] = new
-            state[1, slot, here, :] = moment
-            state[2, slot, here, :] = spread
-            wide[chip, q, here, :] = new.astype(jnp.bfloat16)
+            write(0, new)
+            write(1, moment)
+            write(2, spread)
+            wide[chip, q, here] = new.astype(jnp.bfloat16).reshape(block, group, LANES)
 
         @pl.when(chip > 0)
         def _():
@@ -381,31 +451,39 @@
                 state_store(i, q - 1).wait()
                 state_load(i, q - 1 + STATE_SLOTS).start()
 
-    @pl.loop(1, C)
-    def _(far):
-        @pl.loop(0, d.PQ)
-        def _(q):
-            @pl.when(chip - far >= 0)
-            def _():
-                ag_copy(0, chip - far, q).wait_recv()
-
-                @pl.when(chip < C - 1)
-                def _():
-                    ag_copy(0, chip - far, q).start()
-
-                local_copy(chip - far, q).start()
-                partner_copy(chip - far, q).start()
-
-            @pl.when(chip + far < C)
-            def _():
-                ag_copy(1, chip + far, q).wait_recv()
-
-                @pl.when(chip > 0)
-                def _():
-                    ag_copy(1, chip + far, q).start()
-
-                local_copy(chip + far, q).start()
-                partner_copy(chip + far, q).start()
+    def pass_on(way, c, q):
+        ag_copy(way, c, q).wait_recv()
+
+        @pl.when(chip < C - 1 if way == 0 else chip > 0)
+        def _():
+            ag_copy(way, c, q).start()
+
+        local_copy(c, q).start()
+        partner_copy(c, q).start()
+
+    def relay(way, t):
+        room = chip if way == 0 else C - 1 - chip
+        chunk, q = (t - BEHIND) // (d.PQ + BEHIND), lax.rem(t - BEHIND, d.PQ + BEHIND)
+        near = chip - 1 - chunk if way == 0 else chip + 1 + chunk
+
+        @pl.when((t >= BEHIND) & (chunk < room - 1) & (q < d.PQ))
+        def _():
+            pass_on(way, near, q)
+
+        late = t - jnp.maximum(room - 1, half - 1) * d.PQ - BEHIND * room
+
+        @pl.when((room > 0) & (late >= 0) & (late < d.PQ))
+        def _():
+            pass_on(way, 0 if way == 0 else C - 1, late)
+
+    @pl.loop(0, (C - 1) * (d.PQ + BEHIND))
+    def _(u):
+        @pl.when(u < d.PQ)
+        def _():
+            update(u)
+
+        relay(0, u)
+        relay(1, u)
 
     for q in range(max(0, d.PQ - STATE_SLOTS), d.PQ):
         for i in range(3):
@@ -417,21 +495,28 @@
         for j in range(NB):
             b_remote(l, j).wait_send()
 
-    @pl.loop(1, count)
-    def _(k):
-        norm_copy(k, me).wait_send()
-
-    @pl.loop(0, C - 1)
-    def _(s):
-        @pl.loop(0, pieces)
-        def _(p):
-            @pl.when(chip < C - 1 - s)
-            def _():
-                rs_copy(0, s, p).wait_send()
-
-            @pl.when(chip > s)
-            def _():
-                rs_copy(1, s, p).wait_send()
+    @pl.when(at_end)
+    def _():
+        @pl.loop(1, count)
+        def _(k):
+            norm_copy(k, me).wait_send()
+
+    @pl.loop(steps - min(FLIGHT, steps), steps)
+    def _(n):
+        @pl.when(chip < C - 1)
+        def _():
+            rs_copy(0, n // pieces, lax.rem(n, pieces)).wait_send()
+
+        @pl.when(chip > 0)
+        def _():
+            rs_copy(1, n // pieces, lax.rem(n, pieces)).wait_send()
+
+    @pl.loop(totals - min(FLIGHT, totals), totals)
+    def _(n):
+        for way in range(2):
+            @pl.when(at_sink(way))
+            def _():
+                tot_copy(way, n // pieces, lax.rem(n, pieces)).wait_send()
 
     @pl.loop(0, C)
     def _(c):
@@ -464,32 +549,37 @@
     d.AW = d.R if d.R % LANES == 0 else CORES * d.R
     d.WC = math.gcd(512, d.N)
     d.NB = d.N // d.WC
-    d.PQ = 8
+    d.PQ = d.NB * SPLIT
     pieces = d.L * d.NB
     tiles = d.R // TILE * (d.WC // LANES)
-    rows = d.R * d.L * d.N // LANES
-    d.rows_q = rows // d.PQ
+    across = d.L * d.N // LANES
+    group = d.L * d.WC // LANES
     count = d.n_tp * d.n_dp
+    half = d.C // 2
+    packed = (tiles + 1, TILE, LANES)
     hbm = pl.BlockSpec(memory_space=pl.ANY)
     dma = pltpu.SemaphoreType.DMA
-    flat = jax.ShapeDtypeStruct((rows, LANES), jnp.float32)
+    flat = jax.ShapeDtypeStruct((d.R, across, LANES), jnp.float32)
     return pl.pallas_call(
         functools.partial(step_kernel, d),
-        out_shape=(flat, flat, flat, jax.ShapeDtypeStruct((d.n_dp * rows, LANES), jnp.bfloat16)),
+        out_shape=(flat, flat, flat, jax.ShapeDtypeStruct((d.n_dp * d.R, across, LANES), jnp.bfloat16)),
         in_specs=[hbm] * 5,
         out_specs=[hbm] * 4,
         scratch_shapes=[
             pltpu.VMEM((CORES, d.L, d.C, d.T, d.AW), jnp.bfloat16),
             pltpu.VMEM((CORES, d.L, d.NB, d.T, d.WC), jnp.bfloat16),
             pltpu.VMEM((d.R, d.WC), jnp.float32),
-            pltpu.VMEM((2, d.C - 1, pieces, tiles + 1, TILE, LANES), jnp.bfloat16),
-            pltpu.VMEM((rows, LANES), jnp.float32),
-            pltpu.VMEM((d.C, d.PQ, d.rows_q, LANES), jnp.bfloat16),
-            pltpu.VMEM((3, STATE_SLOTS, d.rows_q, LANES), jnp.float32),
+            pltpu.VMEM((2, half, pieces) + packed, jnp.bfloat16),
+            pltpu.VMEM((pieces,) + packed, jnp.bfloat16),
+            pltpu.VMEM((d.NB * d.R * group, LANES), jnp.float32),
+            pltpu.VMEM((d.C, d.PQ, d.R // SPLIT, group, LANES), jnp.bfloat16),
+            pltpu.VMEM((3, STATE_SLOTS, d.R // SPLIT, group, LANES), jnp.float32),
+            pltpu.VMEM((TILE, LANES), jnp.float32),
             pltpu.VMEM((count, 1, LANES), jnp.float32),
             dma((d.L, d.C)), dma((d.L, d.C)), dma((d.L, d.C)),
             dma((d.L, d.NB)), dma((d.L, d.NB)), dma((d.L, d.NB)),
-            dma((2, d.C - 1, pieces)), dma((2, d.C - 1, pieces)),
+            dma((2, half, pieces)), dma((2, half, pieces)),
+            dma((half, pieces)), dma((pieces,)),
             dma((count,)), dma((count,)),
             dma((3, STATE_SLOTS)), dma((3, STATE_SLOTS)),
             dma((2, d.C, d.PQ)), dma((d.C, d.PQ)),
@@ -504,7 +594,7 @@
 
 def to_rows(x):
     r, l, n = x.shape
-    return x.reshape(r, l, n // LANES, LANES).transpose(0, 2, 1, 3).reshape(-1, LANES)
+    return x.reshape(r, l, n // LANES, LANES).transpose(0, 2, 1, 3).reshape(r, -1, LANES)
 
 
 def from_rows(y, l, n):

time: 324 us -> 309 us (0.954)
  Pallas kernels: 301 us -> 285 us
    pallas_call x1, Pallas kernels: 301 us -> 285 us  [whole_step(): pl.pallas_call(functools.partial(step_kernel, d), out_shape=(flat, flat,...]
where the time goes in v3:
time: 309 us
  Pallas kernels  285 us (92%)
  local copies, waits for them, and re-layouts  22.5 us (7%)
    pallas_call x1, Pallas kernels, whole_step(): pl.pallas_call(functools.partial(step_kernel, d), out_shape=(flat, flat,...  285 us
    unnamed x8, local copies, waits for them, and re-layouts  22.5 us

profile of v3, /device:TPU:0, one launch (start us, length us, event | category | flops | bytes accessed | tf_op | source)
XLA Modules:
  0.0 308.6 jit_solution(8797142357328925813)
XLA Ops:
  0.6 285.5 %whole_step.1 = (f32[256,32,128]{2,1,0:T(8,128)}, f32[256,32,128]{2,1,0:T(8,128)}, f32[256,32,128]{2,1,0:T(8,128)}, bf16[2048,32,128]{2,1,0:T(8,128)(2,1)}) custom-call(bf16[2,1024,2048]{2,1,0:T(8,128)(2,1)} %acts.1, bf16[2,1024,2048]{2,1,0:T(8,128)(2,1)} %grads.1, f32[256,32,128]{2,1,0:T(8,128)} %bitcast.36, f32[256,32,128]{2,1,0:T(8,128)} %bitcast.37, ...), custom_call_target="tpu_custom_call" | custom-call | tf_op jit(solution)/shard_map/whole_step/pallas_call | solution.py:563
  286.1 0.0 copy-start.1
  286.1 6.3 %copy.20 = f32[256,2,2048]{2,1,0:T(2,128)} copy(f32[256,2,2048]{2,1,0:T(2,128)} %bitcast.41) | data formatting | bytes 8388608
  292.4 0.0 copy-start
  292.4 6.5 %copy.21 = f32[256,2,2048]{2,1,0:T(2,128)} copy(f32[256,2,2048]{2,1,0:T(2,128)} %bitcast.40) | data formatting | bytes 8388608
  298.9 0.0 copy-done.1
  298.9 2.1 copy.22
  301.1 1.4 copy-done
  302.5 6.2 %copy.23 = bf16[2048,2,2048]{2,1,0:T(2,128)(2,1)} copy(bf16[2048,2,2048]{2,1,0:T(2,128)(2,1)S(1)} %bitcast.35) | data formatting | bytes 33554432
Async XLA Ops:
  286.1 12.8 %copy-start.1 = (f32[256,32,128]{2,1,0:T(8,128)S(1)}, f32[256,32,128]{2,1,0:T(8,128)}, u32[]{:S(2)}) copy-start(f32[256,32,128]{2,1,0:T(8,128)} %get-tuple-element.10) | copy-start | bytes 12582916
  292.4 10.1 %copy-start = (bf16[2048,32,128]{2,1,0:T(8,128)(2,1)S(1)}, bf16[2048,32,128]{2,1,0:T(8,128)(2,1)}, u32[]{:S(2)}) copy-start(bf16[2048,32,128]{2,1,0:T(8,128)(2,1)} %get-tuple-element.11) | copy-start | bytes 50331652

commit v4 on v3

--- a/solution.py
+++ b/solution.py
@@ -25,6 +25,7 @@
 LAG = 2
 SPLIT = 2
 BEHIND = 3
+EARLY, MIDDLE = 3, 3
 FLIGHT = 2
 
 
@@ -56,8 +57,9 @@
 ):
     L, T, R, N, C, AW, WC, NB = d.L, d.T, d.R, d.N, d.C, d.AW, d.WC, d.NB
     n_tp, n_dp = d.n_tp, d.n_dp
-    pieces, tiles_across, lane_tiles = L * NB, WC // LANES, N // LANES
-    tiles = R // TILE * tiles_across
+    SP, RP = d.SP, d.RP
+    pieces, tiles_across, lane_tiles = L * NB * SP, WC // LANES, N // LANES
+    tiles = RP // TILE * tiles_across
     group = tiles_across * L
     half, rows_u = C // 2, R // SPLIT
     index = lax.axis_index("dp")
@@ -151,10 +153,16 @@
         for i in range(3):
             state_load(i, jnp.int32(q)).start()
 
-    def product(c, l, j):
+    def parts_of(p):
+        return lax.rem(p, L), p // (L * SP), lax.rem(p // L, SP)
+
+    def product(c, l, j, h):
         total = None
         for w in range(CORES):
-            lhs = a_buf[w, l, c]
+            if SP == 1:
+                lhs = a_buf[w, l, c]
+            else:
+                lhs = a_buf[w, l, c, :, pl.ds(pl.multiple_of(h * RP, LANES), RP)]
             if AW != R:
                 lhs = jnp.where(core == 0, lhs[:, :R], lhs[:, R:])
             term = lax.dot_general(
@@ -176,7 +184,7 @@
         rs_copy(way, s, p).wait_recv()
         scale = rx[way, s, p, tiles].astype(jnp.float32) * (1.0 / TOP)
 
-        @pl.loop(0, R // TILE)
+        @pl.loop(0, RP // TILE)
         def _(r):
             rows = pl.ds(pl.multiple_of(r * TILE, TILE), TILE)
             for t in range(tiles_across):
@@ -191,29 +199,29 @@
                 top = jnp.maximum(top, jnp.abs(part[rows, pl.ds(t * LANES, LANES)]))
             return top
 
-        top = lax.fori_loop(0, R // TILE, widest, jnp.zeros((TILE, LANES), jnp.float32))
+        top = lax.fori_loop(0, RP // TILE, widest, jnp.zeros((TILE, LANES), jnp.float32))
         top = jnp.maximum(top, 1e-25).astype(jnp.bfloat16)
         rx[way, s, p, tiles] = top
         shrink = TOP / top.astype(jnp.float32)
 
-        @pl.loop(0, R // TILE)
+        @pl.loop(0, RP // TILE)
         def _(r):
             rows = pl.ds(pl.multiple_of(r * TILE, TILE), TILE)
             for t in range(tiles_across):
                 value = part[rows, pl.ds(t * LANES, LANES)]
                 rx[way, s, p, r * tiles_across + t] = encode(value, shrink)
 
-    def put(r, l, j, t, value):
+    def put(r, l, j, h, t, value):
         for k in range(TILE // 8):
-            start = (j * R + r * TILE + k * 8) * group + t * L + l
+            start = (j * R + h * RP + r * TILE + k * 8) * group + t * L + l
             grad[pl.ds(start, 8, stride=group), :] = value[k * 8 : k * 8 + 8]
 
-    def keep_part(l, j):
-        @pl.loop(0, R // TILE)
+    def keep_part(l, j, h):
+        @pl.loop(0, RP // TILE)
         def _(r):
             rows = pl.ds(pl.multiple_of(r * TILE, TILE), TILE)
             for t in range(tiles_across):
-                put(r, l, j, t, part[rows, pl.ds(t * LANES, LANES)])
+                put(r, l, j, h, t, part[rows, pl.ds(t * LANES, LANES)])
 
     def add_squares():
         def square(r, sums):
@@ -223,7 +231,7 @@
                 sums = sums + x * x
             return sums
 
-        squares[...] = lax.fori_loop(0, R // TILE, square, squares[...])
+        squares[...] = lax.fori_loop(0, RP // TILE, square, squares[...])
 
     def owner_of(way, s):
         return half + s if way == 0 else half - 1 - s
@@ -241,11 +249,11 @@
         hops = chip if way == 0 else C - 1 - chip
         n = t - LAG * hops
         s, p = n // pieces, lax.rem(n, pieces)
-        l, j = lax.rem(p, L), p // L
+        l, j, h = parts_of(p)
 
         @pl.when((n >= 0) & (n < steps))
         def _():
-            product(owner_of(way, s), l, j)
+            product(owner_of(way, s), l, j, h)
 
             @pl.when(hops > 0)
             def _():
@@ -259,7 +267,7 @@
 
             @pl.when(last)
             def _():
-                keep_part(l, j)
+                keep_part(l, j, h)
 
             @pl.when(jnp.logical_not(last))
             def _():
@@ -276,27 +284,32 @@
 
     totals = (half - 1) * pieces
     leave = max(steps, totals + LAG * (C - 1))
-    in_loop = min(totals, steps + LAG * (C - 1) - leave)
+    early, middle = min(EARLY, totals), min(EARLY + MIDDLE, totals)
 
     def at_sink(way):
         return chip == (C - 1 if way == 0 else 0)
 
-    def send_total(n):
+    def wait_total(n):
         for way in range(2):
             @pl.when(at_sink(way))
             def _():
-                @pl.when(n >= FLIGHT)
+                tot_copy(way, n // pieces, lax.rem(n, pieces)).wait_send()
+
+    def send_totals(first_one, stop, gated):
+        @pl.loop(first_one, stop)
+        def _(n):
+            if gated:
+                wait_total(n - FLIGHT)
+            for way in range(2):
+                @pl.when(at_sink(way))
                 def _():
-                    before = n - FLIGHT
-                    tot_copy(way, before // pieces, lax.rem(before, pieces)).wait_send()
-
-                tot_copy(way, n // pieces, lax.rem(n, pieces)).start()
+                    tot_copy(way, n // pieces, lax.rem(n, pieces)).start()
 
     @pl.loop(0, steps + LAG * (C - 1))
     def _(t):
-        l, j = lax.rem(t, L), t // L
-
-        @pl.when(t < pieces)
+        l, j, h = parts_of(t)
+
+        @pl.when((t < pieces) & (h == 0))
         def _():
             @pl.when(j == 0)
             def _():
@@ -317,9 +330,9 @@
         stream(0, t)
         stream(1, t)
 
-        @pl.when((t >= leave) & (t < leave + in_loop))
-        def _():
-            send_total(t - leave)
+        @pl.when(t == leave)
+        def _():
+            send_totals(0, early, False)
 
     norm[me] = jnp.sum(squares[...], axis=0, keepdims=True)
 
@@ -341,15 +354,15 @@
         def _(k):
             norm_copy(k, me).start()
 
+    send_totals(early, middle, False)
+
     @pl.loop(1, count)
     def _(k):
         @pl.when(from_end(k))
         def _():
             norm_copy(k, lax.rem(me - k + count, count)).wait_recv()
 
-    @pl.loop(in_loop, totals)
-    def _(n):
-        send_total(n)
+    send_totals(middle, totals, True)
 
     total = None
     for a in range(n_tp):
@@ -394,17 +407,18 @@
     def update(q):
         slot, j = lax.rem(q, STATE_SLOTS), q // SPLIT
 
-        @pl.when(jnp.logical_not(at_end) & (lax.rem(q, SPLIT) == 0))
+        @pl.when(jnp.logical_not(at_end) & (lax.rem(q, SPLIT // SP) == 0))
         def _():
             for l in range(L):
-                p = j * L + l
+                p = q // (SPLIT // SP) * L + l
+                h = lax.rem(q, SP)
                 tot_copy(0, 0, p).wait_recv()
                 scale = tot[p, tiles].astype(jnp.float32) * (1.0 / TOP)
 
-                @pl.loop(0, R // TILE)
+                @pl.loop(0, RP // TILE)
                 def _(r):
                     for t in range(tiles_across):
-                        put(r, l, j, t, decode(tot[p, r * tiles_across + t], scale))
+                        put(r, l, j, h, t, decode(tot[p, r * tiles_across + t], scale))
 
         for i in range(3):
             state_load(i, q).wait()
@@ -511,12 +525,11 @@
         def _():
             rs_copy(1, n // pieces, lax.rem(n, pieces)).wait_send()
 
-    @pl.loop(totals - min(FLIGHT, totals), totals)
+    @pl.loop(0, totals)
     def _(n):
-        for way in range(2):
-            @pl.when(at_sink(way))
-            def _():
-                tot_copy(way, n // pieces, lax.rem(n, pieces)).wait_send()
+        @pl.when((n < middle - FLIGHT) | (n >= totals - FLIGHT))
+        def _():
+            wait_total(n)
 
     @pl.loop(0, C)
     def _(c):
@@ -550,8 +563,10 @@
     d.WC = math.gcd(512, d.N)
     d.NB = d.N // d.WC
     d.PQ = d.NB * SPLIT
-    pieces = d.L * d.NB
-    tiles = d.R // TILE * (d.WC // LANES)
+    d.SP = SPLIT if d.R % (SPLIT * LANES) == 0 else 1
+    d.RP = d.R // d.SP
+    pieces = d.L * d.NB * d.SP
+    tiles = d.RP // TILE * (d.WC // LANES)
     across = d.L * d.N // LANES
     group = d.L * d.WC // LANES
     count = d.n_tp * d.n_dp
@@ -568,7 +583,7 @@
         scratch_shapes=[
             pltpu.VMEM((CORES, d.L, d.C, d.T, d.AW), jnp.bfloat16),
             pltpu.VMEM((CORES, d.L, d.NB, d.T, d.WC), jnp.bfloat16),
-            pltpu.VMEM((d.R, d.WC), jnp.float32),
+            pltpu.VMEM((d.RP, d.WC), jnp.float32),
             pltpu.VMEM((2, half, pieces) + packed, jnp.bfloat16),
             pltpu.VMEM((pieces,) + packed, jnp.bfloat16),
             pltpu.VMEM((d.NB * d.R * group, LANES), jnp.float32),

time: 309 us -> 291 us (0.942)
  Pallas kernels: 285 us -> 268 us
    pallas_call x1, Pallas kernels: 285 us -> 268 us  [whole_step(): pl.pallas_call(functools.partial(step_kernel, d), out_shape=(flat, flat,...]
where the time goes in v4:
time: 291 us
  Pallas kernels  268 us (92%)
  local copies, waits for them, and re-layouts  22.5 us (8%)
    pallas_call x1, Pallas kernels, whole_step(): pl.pallas_call(functools.partial(step_kernel, d), out_shape=(flat, flat,...  268 us
    unnamed x8, local copies, waits for them, and re-layouts  22.5 us

profile of v4, /device:TPU:0, one launch (start us, length us, event | category | flops | bytes accessed | tf_op | source)
XLA Modules:
  0.0 290.8 jit_solution(12307633464877366268)
XLA Ops:
  0.6 267.7 %whole_step.1 = (f32[256,32,128]{2,1,0:T(8,128)}, f32[256,32,128]{2,1,0:T(8,128)}, f32[256,32,128]{2,1,0:T(8,128)}, bf16[2048,32,128]{2,1,0:T(8,128)(2,1)}) custom-call(bf16[2,1024,2048]{2,1,0:T(8,128)(2,1)} %acts.1, bf16[2,1024,2048]{2,1,0:T(8,128)(2,1)} %grads.1, f32[256,32,128]{2,1,0:T(8,128)} %bitcast.36, f32[256,32,128]{2,1,0:T(8,128)} %bitcast.37, ...), custom_call_target="tpu_custom_call" | custom-call | tf_op jit(solution)/shard_map/whole_step/pallas_call | solution.py:578
  268.3 0.0 copy-start.1
  268.3 6.3 %copy.20 = f32[256,2,2048]{2,1,0:T(2,128)} copy(f32[256,2,2048]{2,1,0:T(2,128)} %bitcast.41) | data formatting | bytes 8388608
  274.6 0.0 copy-start
  274.6 6.5 %copy.21 = f32[256,2,2048]{2,1,0:T(2,128)} copy(f32[256,2,2048]{2,1,0:T(2,128)} %bitcast.40) | data formatting | bytes 8388608
  281.1 0.0 copy-done.1
  281.1 2.1 copy.22
  283.2 1.4 copy-done
  284.7 6.2 %copy.23 = bf16[2048,2,2048]{2,1,0:T(2,128)(2,1)} copy(bf16[2048,2,2048]{2,1,0:T(2,128)(2,1)S(1)} %bitcast.35) | data formatting | bytes 33554432
Async XLA Ops:
  268.3 12.8 %copy-start.1 = (f32[256,32,128]{2,1,0:T(8,128)S(1)}, f32[256,32,128]{2,1,0:T(8,128)}, u32[]{:S(2)}) copy-start(f32[256,32,128]{2,1,0:T(8,128)} %get-tuple-element.10) | copy-start | bytes 12582916
  274.6 10.1 %copy-start = (bf16[2048,32,128]{2,1,0:T(8,128)(2,1)S(1)}, bf16[2048,32,128]{2,1,0:T(8,128)(2,1)}, u32[]{:S(2)}) copy-start(bf16[2048,32,128]{2,1,0:T(8,128)(2,1)} %get-tuple-element.11) | copy-start | bytes 50331652

commit v5 on v4

--- a/solution.py
+++ b/solution.py
@@ -26,6 +26,7 @@
 SPLIT = 2
 BEHIND = 3
 EARLY, MIDDLE = 3, 3
+TAIL = 3
 FLIGHT = 2
 
 
@@ -49,11 +50,11 @@
 def step_kernel(
     d,
     acts, grads, master, first, second,
-    new_master, new_first, new_second, weights,
+    new_master, new_first, new_second, weights, tail,
     a_buf, b_buf, part, rx, tot, grad, wide, state, squares, norm,
     a_own, a_send, a_recv, b_own, b_send, b_recv,
     rs_send, rs_recv, tot_send, tot_recv, norm_send, norm_recv, state_in, state_out,
-    ag_send, ag_recv, out_local, out_send, out_recv,
+    ag_send, ag_recv, out_local, out_send, out_recv, tail_sem,
 ):
     L, T, R, N, C, AW, WC, NB = d.L, d.T, d.R, d.N, d.C, d.AW, d.WC, d.NB
     n_tp, n_dp = d.n_tp, d.n_dp
@@ -404,6 +405,29 @@
             device_id=partner, device_id_type=MESH,
         )
 
+    first_tail = d.PQ - d.TAIL
+
+    def is_tail(way, c, q, at):
+        if way == 0:
+            return (q >= first_tail) & (c == 0) & (at == C - 2)
+        return (q >= first_tail) & (c == C - 1) & (at == 1)
+
+    def tail_copy(c, q):
+        return pltpu.make_async_copy(
+            wide.at[c, q], tail.at[q - first_tail], tail_sem.at[q - first_tail]
+        )
+
+    def hand_on(way, c, q):
+        left = is_tail(way, c, q, chip)
+
+        @pl.when((chip < C - 1 if way == 0 else chip > 0) & jnp.logical_not(left))
+        def _():
+            ag_copy(way, c, q).start()
+
+        @pl.when(left)
+        def _():
+            tail_copy(c, q).start()
+
     def update(q):
         slot, j = lax.rem(q, STATE_SLOTS), q // SPLIT
 
@@ -446,14 +470,8 @@
             write(2, spread)
             wide[chip, q, here] = new.astype(jnp.bfloat16).reshape(block, group, LANES)
 
-        @pl.when(chip > 0)
-        def _():
-            ag_copy(1, chip, q).start()
-
-        @pl.when(chip < C - 1)
-        def _():
-            ag_copy(0, chip, q).start()
-
+        hand_on(1, chip, q)
+        hand_on(0, chip, q)
         for i in range(3):
             state_store(i, q).start()
         local_copy(chip, q).start()
@@ -466,14 +484,12 @@
                 state_load(i, q - 1 + STATE_SLOTS).start()
 
     def pass_on(way, c, q):
-        ag_copy(way, c, q).wait_recv()
-
-        @pl.when(chip < C - 1 if way == 0 else chip > 0)
-        def _():
-            ag_copy(way, c, q).start()
-
-        local_copy(c, q).start()
-        partner_copy(c, q).start()
+        @pl.when(jnp.logical_not(is_tail(way, c, q, chip - 1 if way == 0 else chip + 1)))
+        def _():
+            ag_copy(way, c, q).wait_recv()
+            hand_on(way, c, q)
+            local_copy(c, q).start()
+            partner_copy(c, q).start()
 
     def relay(way, t):
         room = chip if way == 0 else C - 1 - chip
@@ -535,17 +551,25 @@
     def _(c):
         @pl.loop(0, d.PQ)
         def _(q):
-            @pl.when((c <= chip) & (chip < C - 1))
-            def _():
-                ag_copy(0, c, q).wait_send()
-
-            @pl.when((c >= chip) & (chip > 0))
-            def _():
-                ag_copy(1, c, q).wait_send()
-
-            local_copy(c, q).wait()
-            partner_copy(c, q).wait_send()
-            partner_arrival(c, q).wait_recv()
+            for way in range(2):
+                left = is_tail(way, c, q, chip)
+                sent = (c <= chip) & (chip < C - 1) if way == 0 else (c >= chip) & (chip > 0)
+
+                @pl.when(sent & jnp.logical_not(left))
+                def _():
+                    ag_copy(way, c, q).wait_send()
+
+                @pl.when(left)
+                def _():
+                    tail_copy(c, q).wait()
+
+            missing = is_tail(0, c, q, chip - 1) | is_tail(1, c, q, chip + 1)
+
+            @pl.when(jnp.logical_not(missing))
+            def _():
+                local_copy(c, q).wait()
+                partner_copy(c, q).wait_send()
+                partner_arrival(c, q).wait_recv()
 
 
 class Sizes:
@@ -563,6 +587,7 @@
     d.WC = math.gcd(512, d.N)
     d.NB = d.N // d.WC
     d.PQ = d.NB * SPLIT
+    d.TAIL = min(TAIL, d.PQ)
     d.SP = SPLIT if d.R % (SPLIT * LANES) == 0 else 1
     d.RP = d.R // d.SP
     pieces = d.L * d.NB * d.SP
@@ -575,11 +600,15 @@
     hbm = pl.BlockSpec(memory_space=pl.ANY)
     dma = pltpu.SemaphoreType.DMA
     flat = jax.ShapeDtypeStruct((d.R, across, LANES), jnp.float32)
-    return pl.pallas_call(
+    outs = pl.pallas_call(
         functools.partial(step_kernel, d),
-        out_shape=(flat, flat, flat, jax.ShapeDtypeStruct((d.n_dp * d.R, across, LANES), jnp.bfloat16)),
+        out_shape=(
+            flat, flat, flat,
+            jax.ShapeDtypeStruct((d.n_dp * d.R, across, LANES), jnp.bfloat16),
+            jax.ShapeDtypeStruct((d.TAIL, d.R // SPLIT, group, LANES), jnp.bfloat16),
+        ),
         in_specs=[hbm] * 5,
-        out_specs=[hbm] * 4,
+        out_specs=[hbm] * 5,
         scratch_shapes=[
             pltpu.VMEM((CORES, d.L, d.C, d.T, d.AW), jnp.bfloat16),
             pltpu.VMEM((CORES, d.L, d.NB, d.T, d.WC), jnp.bfloat16),
@@ -599,12 +628,89 @@
             dma((3, STATE_SLOTS)), dma((3, STATE_SLOTS)),
             dma((2, d.C, d.PQ)), dma((d.C, d.PQ)),
             dma((d.C, d.PQ)), dma((d.C, d.PQ)), dma((d.C, d.PQ)),
+            dma((d.TAIL,)),
         ],
         compiler_params=pltpu.CompilerParams(
             collective_id=0, has_side_effects=True, vmem_limit_bytes=67043328
         ),
         name="whole_step",
     )(acts, grads, master, first, second)
+    return d, outs
+
+
+def copy_kernel(count, *refs):
+    sources, targets = refs[:count], refs[count : 2 * count]
+    for source, target in zip(sources, targets):
+        target[...] = source[...]
+
+
+def copy_out(arrays):
+    blocks = 8
+
+    def spec(x):
+        return pl.BlockSpec((x.shape[0] // blocks,) + x.shape[1:], lambda b: (b, 0, 0))
+
+    moved = 2 * sum(x.size * x.dtype.itemsize for x in arrays)
+    return pl.pallas_call(
+        functools.partial(copy_kernel, len(arrays)),
+        grid=(blocks,),
+        out_shape=[jax.ShapeDtypeStruct(x.shape, x.dtype) for x in arrays],
+        in_specs=[spec(x) for x in arrays],
+        out_specs=[spec(x) for x in arrays],
+        cost_estimate=pl.CostEstimate(flops=0, bytes_accessed=moved, transcendentals=0),
+        compiler_params=pltpu.CompilerParams(vmem_limit_bytes=56 * 2**20),
+        name="copy_out",
+    )(*arrays)
+
+
+def insert_kernel(d, own, other, before, weights, sems):
+    index = lax.axis_index("dp")
+    chip, core = index // CORES, lax.rem(index, CORES)
+    group, rows_u = own.shape[2], own.shape[1]
+
+    def each(act):
+        for n, source in enumerate((own, other)):
+            for k in range(d.TAIL):
+                q = d.PQ - d.TAIL + k
+                c = jnp.where(chip == 0, d.C - 1, 0)
+                row = (c * CORES + (core if n == 0 else 1 - core)) * d.R + q % SPLIT * rows_u
+                copy = pltpu.make_async_copy(
+                    source.at[k],
+                    weights.at[pl.ds(row, rows_u), pl.ds(q // SPLIT * group, group)],
+                    sems.at[n, k],
+                )
+                copy.start() if act == 0 else copy.wait()
+
+    @pl.when((chip == 0) | (chip == d.C - 1))
+    def _():
+        each(0)
+        each(1)
+
+
+def insert(d, own, other, weights):
+    hbm, vmem = pl.BlockSpec(memory_space=pl.ANY), pl.BlockSpec(memory_space=pltpu.VMEM)
+    return pl.pallas_call(
+        functools.partial(insert_kernel, d),
+        out_shape=jax.ShapeDtypeStruct(weights.shape, weights.dtype),
+        in_specs=[vmem, vmem, hbm],
+        out_specs=hbm,
+        input_output_aliases={2: 0},
+        scratch_shapes=[pltpu.SemaphoreType.DMA((2, d.TAIL))],
+        name="insert",
+    )(own, other, weights)
+
+
+def finish(d, outs):
+    *arrays, tail = outs
+    last = d.C - 1
+    hops = [(1, 0), (last - 1, last)]
+    pairs = [(a * CORES + k, b * CORES + k) for a, b in hops for k in range(CORES)]
+    swap = [(b * CORES + k, b * CORES + 1 - k) for _, b in hops for k in range(CORES)]
+    own = lax.ppermute(tail, "dp", pairs)
+    arrays = copy_out(arrays)
+    own, arrays = lax.optimization_barrier((own, arrays))
+    other = lax.ppermute(own, "dp", swap)
+    return *arrays[:3], insert(d, own, other, arrays[3])
 
 
 def to_rows(x):
@@ -618,7 +724,7 @@
 
 def on_device(activations, out_grads, master, first_moment, second_moment):
     states = [to_rows(x) for x in (master, first_moment, second_moment)]
-    outs = whole_step(activations, out_grads, *states)
+    outs = finish(*whole_step(activations, out_grads, *states))
     return tuple(from_rows(y, *master.shape[1:]) for y in outs)
 
 

time: 291 us -> 281 us (0.966)
  local copies, waits for them, and re-layouts: 22.5 us -> 0.9 us
  Pallas kernels: 268 us -> 274 us
  starting transfers between devices: 0 us -> 3.44 us
    pallas_call x0 -> x2, Pallas kernels: none -> 23 us  [the longest x1 20.5 us: copy_out(): pl.pallas_call(functools.partial(copy_kernel, len(arrays)), grid=(blocks,...]
    unnamed x8 -> x4, local copies, waits for them, and re-layouts: 22.5 us -> 0.9 us
    pallas_call x1, Pallas kernels: 268 us -> 251 us  [whole_step(): pl.pallas_call(functools.partial(step_kernel, d), out_shape=(flat, flat,...]
    ppermute x0 -> x2, starting transfers between devices: none -> 3.44 us  [the longest x1 2.15 us: finish(): other = lax.ppermute(own, 'dp', swap)]
  transfers between devices with their start and end apart: 0 -> 2, of which waited for: 0 -> 2; matrix products, arithmetic and copies ran while one was open for 0% -> 0% of each run, Pallas kernels for 0% -> 7%
where the time goes in v5:
time: 281 us
  Pallas kernels  274 us (98%)
  starting transfers between devices  3.44 us (1%)
    pallas_call x1, Pallas kernels, whole_step(): pl.pallas_call(functools.partial(step_kernel, d), out_shape=(flat, flat,...  251 us
    pallas_call x1, Pallas kernels, copy_out(): pl.pallas_call(functools.partial(copy_kernel, len(arrays)), grid=(blocks,...  20.5 us
  transfers between devices with their start and end apart: 2, of which 2 were waited for; matrix products, arithmetic and copies ran while one was open for 0% of the time, Pallas kernels for 7%

profile of v5, /device:TPU:0, one launch (start us, length us, event | category | flops | bytes accessed | tf_op | source)
XLA Modules:
  0.0 281.0 jit_solution(9171229259407058349)
XLA Ops:
  0.6 250.9 %whole_step.1 = (f32[256,32,128]{2,1,0:T(8,128)}, f32[256,32,128]{2,1,0:T(8,128)}, f32[256,32,128]{2,1,0:T(8,128)}, bf16[2048,32,128]{2,1,0:T(8,128)(2,1)}, bf16[3,128,8,128]{3,2,1,0:T(8,128)(2,1)}) custom-call(bf16[2,1024,2048]{2,1,0:T(8,128)(2,1)} %acts.1, bf16[2,1024,2048]{2,1,0:T(8,128)(2,1)} %grads.1, f32[256,32,128]{2,1,0:T(8,128)} %bitcast.36, ...), custom_call_target="tpu_custom_call" | custom-call | tf_op jit(solution)/shard_map/whole_step/pallas_call | solution.py:603
  251.5 1.3 collective-permute-start
  252.8 20.5 %copy_out.1 = (f32[256,32,128]{2,1,0:T(8,128)}, f32[256,32,128]{2,1,0:T(8,128)}, f32[256,32,128]{2,1,0:T(8,128)}, bf16[2048,32,128]{2,1,0:T(8,128)(2,1)}) custom-call(f32[256,32,128]{2,1,0:T(8,128)} %get-tuple-element.19.refs_0_, f32[256,32,128]{2,1,0:T(8,128)} %get-tuple-element.20.refs_1_, f32[256,32,128]{2,1,0:T(8,128)} %get-tuple-element.21.refs_2_, ...), custom_call_target="tpu_custom_call" | custom-call | bytes 58720256 | tf_op jit(solution)/shard_map/copy_out/pallas_call | solution.py:654
  273.3 0.1 collective-permute-done.own
  273.4 0.0 copy-start
  273.4 2.1 collective-permute-start.1
  275.6 2.0 collective-permute-done.1.other
  277.6 0.0 copy-done
  277.6 0.0 copy-start.1
  277.6 0.9 copy-done.1
  278.5 2.6 insert.1
Async XLA Ops:
  251.5 21.9 %collective-permute-start = (bf16[3,128,8,128]{3,2,1,0:T(8,128)(2,1)}, bf16[3,128,8,128]{3,2,1,0:T(8,128)(2,1)S(1)}, u32[]{:S(2)}, u32[]{:S(2)}) collective-permute-start(bf16[3,128,8,128]{3,2,1,0:T(8,128)(2,1)} %get-tuple-element.18), channel_id=1, source_target_pairs={{2,0},{3,1},{4,6},{5,7},{10,8},{11,9},{12,14},{13,15},{18,16},{19,... | collective-permute-start | bytes 2359304 | tf_op jit(solution)/shard_map/ppermute | solution.py:709
  273.4 4.2 %copy-start = (bf16[3,128,8,128]{3,2,1,0:T(8,128)(2,1)}, bf16[3,128,8,128]{3,2,1,0:T(8,128)(2,1)S(1)}, u32[]{:S(2)}) copy-start(bf16[3,128,8,128]{3,2,1,0:T(8,128)(2,1)S(1)} %collective-permute-done.own) | copy-start | bytes 2359300
  273.4 4.2 %collective-permute-start.1 = (bf16[3,128,8,128]{3,2,1,0:T(8,128)(2,1)S(1)}, bf16[3,128,8,128]{3,2,1,0:T(8,128)(2,1)S(1)}, u32[]{:S(2)}, u32[]{:S(2)}) collective-permute-start(bf16[3,128,8,128]{3,2,1,0:T(8,128)(2,1)S(1)} %collective-permute-done.own), channel_id=1, source_target_pairs={{0,1},{1,0},{6,7},{7,6},{8,9},{9,8},{14,15},{15,14},{16,17},{17,16... | collective-permute-start | bytes 2359304 | tf_op jit(solution)/shard_map/ppermute | solution.py:712
  277.6 0.9 copy-start.1
